TPU v7x, 32 devices: a whole 2x2x4 slice. The times are simulated.
32 devices in a mesh: grp: 2 (over y), lay: 4 (over z), wid: 2 (over x), rep: 2 (over core).
Axes of the slice: x: 2, y: 2, z: 4, core: 2. Of those that a mesh axis runs over, the one named last changes fastest.
Arguments:
- acts: bfloat16 [4, 1024, 2048], P(None, ('grp', 'rep'), 'wid'), parts along dimension 1, may hold values from -6 to 6
- targets: bfloat16 [4, 1024, 2048], P(None, ('grp', 'rep'), 'wid'), parts along dimension 1, may hold values from -6 to 6
- enc_weight: bfloat16 [2048, 8192], P('wid', 'lay'), may hold values from -0.125 to 0.125
- enc_bias: float32 [8192], P('lay'), may hold values from -3 to 3
- gate_mask: int32 [1024, 32], P(('grp', 'rep'), 'lay'), parts along dimension 0, may hold values 0 or 1
- dec_list: int32 [84, 3], P('lay'), may hold values from -1 to 7, as said below
- dec_weight: bfloat16 [84, 256, 2048], P('lay', None, 'wid'), may hold values from -0.125 to 0.125
Outputs:
- grad_enc: float32 [4096, 8192], P(('grp', 'wid'), ('lay', 'rep')), parts along dimension 0
- grad_bias: float32 [16384], P(('grp', 'lay', 'rep')), parts along dimension 0
- grad_dec: float32 [168, 256, 2048], P(('grp', 'lay'), 'rep', 'wid'), parts along dimension 0
There are 2 independent parts, one for each index of `grp`. A program takes and returns all parts, laid end to end along the dimension named above; an argument that names none is the same for every part. Nothing has to cross between parts.
Inputs may be any that keep to these rules, and one draw needn't show every extreme that they name: `dec_list`: each row is (source layer, target layer, latent block within the layer's slab); every triple with source <= target < 4 and block < 8 stands in exactly one row; every other row is (-1, -1, -1).
All inputs are finite; a program needn't handle non-finite values. No bound on the sum of `gate_mask` on one device may be relied on, other than what follows from the above.
Results may differ from a plain program's by a relative error of at most 0.019.
Values may be sent and summed in bfloat16 or wider, within the bound.
A program may use at most 128 MiB of HBM per device.

v0:
```python
import jax
import jax.numpy as jnp
from jax import lax
from jax.experimental import pallas as pl
from jax.experimental.pallas import tpu as pltpu
from jax.sharding import PartitionSpec as P

ROOT = 0.7978845608028654
CUBIC = 0.044715
MESH = pl.DeviceIdType.MESH
BF16 = jnp.bfloat16
F32 = jnp.float32


def smooth_gate(shifted):
    inside_arg = ROOT * (shifted + CUBIC * shifted * shifted * shifted)
    return 0.5 * shifted * (1.0 + jnp.tanh(inside_arg))


def gate_slope(shifted):
    inside_arg = ROOT * (shifted + CUBIC * shifted * shifted * shifted)
    tanh_part = jnp.tanh(inside_arg)
    return 0.5 * (1.0 + tanh_part) + 0.5 * shifted * (1.0 - tanh_part * tanh_part) * ROOT * (
        1.0 + 3.0 * CUBIC * shifted * shifted
    )


def loop(first, count, step):
    if count <= 4:
        for d in range(first, count):
            step(d)
    else:
        lax.fori_loop(first, count, lambda d, c: (step(d), c)[1], 0)


def others(me, count, step):
    loop(1, count, lambda d: step(lax.rem(me + d, count)))


def signal(barrier, **where):
    pl.semaphore_signal(barrier, inc=1, device_id=where, device_id_type=MESH)


def remote(src, dst, send_sem, recv_sem, **where):
    return pltpu.make_async_remote_copy(
        src_ref=src, dst_ref=dst, send_sem=send_sem, recv_sem=recv_sem, device_id=where,
        device_id_type=MESH,
    )


ANY = pl.BlockSpec(memory_space=pl.ANY)


def bounce(src, dst, held, sem):
    into = pltpu.make_async_copy(src, held, sem)
    into.start()
    into.wait()
    out = pltpu.make_async_copy(held, dst, sem)
    out.start()
    return out


def nearest(l, n, step):
    def both(d):
        for j in (l - d, l + d):

            @pl.when((j >= 0) & (j < n))
            def _():
                step(j)

    loop(1, n, both)


def line_gather(l, n, src, slot, send_sem, recv_sem, arrived):
    def own(step):
        @pl.when(l < n - 1)
        def _():
            step(remote(src, slot(l), send_sem.at[l], recv_sem.at[l], lay=l + 1))

        @pl.when(l > 0)
        def _():
            step(remote(src, slot(l), send_sem.at[n], recv_sem.at[l], lay=l - 1))

    def hop(j, step):
        @pl.when((j < l) & (l < n - 1))
        def _():
            step(remote(slot(j), slot(j), send_sem.at[j], recv_sem.at[j], lay=l + 1))

        @pl.when((j > l) & (l > 0))
        def _():
            step(remote(slot(j), slot(j), send_sem.at[j], recv_sem.at[j], lay=l - 1))

    def take(j):
        remote(slot(j), slot(j), send_sem.at[j], recv_sem.at[j], lay=j).wait_recv()
        hop(j, lambda c: c.start())
        arrived(j)

    def finish():
        own(lambda c: c.wait_send())
        nearest(l, n, lambda j: hop(j, lambda c: c.wait_send()))

    own(lambda c: c.start())
    return lambda: nearest(l, n, take), finish


def comm(body, args, outs, sems, cid, held=()):
    return pl.pallas_call(
        body,
        out_shape=tuple(outs),
        in_specs=[ANY] * len(args),
        out_specs=tuple([ANY] * len(outs)),
        scratch_shapes=[pltpu.SemaphoreType.DMA((s,)) for s in sems] + [pltpu.VMEM(*h) for h in held],
        compiler_params=pltpu.CompilerParams(collective_id=cid, has_side_effects=True),
        name=f"exchange_{cid}",
    )(*args)


def exchange(axis, x, out_shape, held_shape, src_of, dst_of, cid):
    n = lax.axis_size(axis)

    def body(x_ref, o_ref, ssem, rsem, lsem, held):
        me = lax.axis_index(axis)
        barrier = pltpu.get_barrier_semaphore()
        others(me, n, lambda j: signal(barrier, **{axis: j}))
        pl.semaphore_wait(barrier, n - 1)

        def send(j):
            return remote(
                src_of(x_ref, j), dst_of(o_ref, me), ssem.at[j], rsem.at[me], **{axis: j}
            )

        def arrival(j):
            return remote(
                src_of(x_ref, me), dst_of(o_ref, j), ssem.at[j], rsem.at[j], **{axis: j}
            )

        others(me, n, lambda j: send(j).start())
        own = bounce(src_of(x_ref, me), dst_of(o_ref, me), held, lsem.at[0])
        others(me, n, lambda j: arrival(j).wait_recv())
        others(me, n, lambda j: send(j).wait_send())
        own.wait()

    return comm(
        body, [x], [jax.ShapeDtypeStruct(out_shape, x.dtype)], (n, n, 1), cid,
        [(held_shape, x.dtype)],
    )[0]


def gather_errors(e, cid):
    n = lax.axis_size("lay")

    def body(e_ref, o_ref, zs, zr, lsem, held):
        l = lax.axis_index("lay")
        barrier = pltpu.get_barrier_semaphore()
        others(l, n, lambda j: signal(barrier, lay=j))
        pl.semaphore_wait(barrier, n - 1)
        take, finish = line_gather(
            l, n, e_ref, lambda j: o_ref.at[:, j], zs, zr, lambda j: None
        )
        own = bounce(e_ref, o_ref.at[:, l], held, lsem.at[0])
        take()
        finish()
        own.wait()

    out = jax.ShapeDtypeStruct((e.shape[0], n) + e.shape[1:], e.dtype)
    return comm(body, [e], [out], (n + 1, n, 1), cid, [(e.shape, e.dtype)])[0]


def gather_latents(h, cid):
    n, w_count = lax.axis_size("lay"), lax.axis_size("wid")
    blocks, toks, width = h.shape

    def body(h_ref, o_ref, zs, zr, xs, xr, lsem, held):
        l, w = lax.axis_index("lay"), lax.axis_index("wid")
        barrier = pltpu.get_barrier_semaphore()
        others(l, n, lambda j: signal(barrier, lay=j))
        others(w, w_count, lambda v: signal(barrier, wid=v))
        pl.semaphore_wait(barrier, n + w_count - 2)

        def slot(j, v):
            return o_ref.at[pl.ds(j * blocks, blocks), v]

        def x_own(v):
            return remote(h_ref, slot(l, w), xs.at[l * w_count + v], xr.at[l * w_count + w], wid=v)

        def x_copy(j, v, source):
            return remote(
                slot(j, source), slot(j, source), xs.at[j * w_count + v],
                xr.at[j * w_count + source], wid=v,
            )

        take, finish = line_gather(
            l, n, h_ref, lambda j: slot(j, w), zs, zr,
            lambda j: others(w, w_count, lambda v: x_copy(j, v, w).start()),
        )
        others(w, w_count, lambda v: x_own(v).start())
        own = bounce(h_ref, slot(l, w), held, lsem.at[0])
        take()
        finish()
        others(w, w_count, lambda v: x_own(v).wait_send())
        nearest(l, n, lambda j: others(w, w_count, lambda v: x_copy(j, v, w).wait_send()))
        loop(0, n, lambda j: others(w, w_count, lambda v: x_copy(j, v, v).wait_recv()))
        own.wait()

    out = jax.ShapeDtypeStruct((n * blocks, w_count, toks, width), h.dtype)
    return comm(
        body, [h], [out], (n + 1, n, n * w_count, n * w_count, 1), cid, [(h.shape, h.dtype)]
    )[0]


def slots_and_twin(slot_err, lat, err, acts_here, cid):
    w_count, r_count = lax.axis_size("wid"), lax.axis_size("rep")
    assert r_count == 2
    slots, _, toks, width = slot_err.shape
    half = width // r_count

    def body(s_ref, l_ref, e_ref, a_ref, so_ref, lo_ref, eo_ref, ao_ref, ssem, rsem, lsem, ts, tr,
             held, held_acts):
        w, r = lax.axis_index("wid"), lax.axis_index("rep")
        twin = 1 - r
        barrier = pltpu.get_barrier_semaphore()
        others(w, w_count, lambda v: signal(barrier, wid=v))
        signal(barrier, rep=twin)
        pl.semaphore_wait(barrier, w_count)

        def send(v):
            return remote(s_ref.at[:, v], so_ref.at[w], ssem.at[v], rsem.at[w], wid=v)

        def arrival(v):
            return remote(s_ref.at[:, w], so_ref.at[v], ssem.at[v], rsem.at[v], wid=v)

        others(w, w_count, lambda v: send(v).start())
        twins = [
            remote(l_ref.at[:, :, pl.ds(pl.multiple_of(twin * half, half), half)], lo_ref,
                   ts.at[0], tr.at[0], rep=twin),
            remote(e_ref, eo_ref, ts.at[1], tr.at[1], rep=twin),
            remote(a_ref, ao_ref.at[r], ts.at[2], tr.at[2], rep=twin),
        ]
        for c in twins:
            c.start()
        own = bounce(s_ref.at[:, w], so_ref.at[w], held, lsem.at[0])
        own_acts = bounce(a_ref, ao_ref.at[r], held_acts, lsem.at[1])
        others(w, w_count, lambda v: arrival(v).wait_recv())
        others(w, w_count, lambda v: send(v).wait_send())
        own.wait()
        own_acts.wait()
        for c in twins:
            c.wait()

    outs = [
        jax.ShapeDtypeStruct((w_count, slots, toks, width), slot_err.dtype),
        jax.ShapeDtypeStruct(lat.shape[:2] + (half,), lat.dtype),
        jax.ShapeDtypeStruct(err.shape, err.dtype),
        jax.ShapeDtypeStruct((r_count,) + acts_here.shape, acts_here.dtype),
    ]
    return comm(body, [slot_err, lat, err, acts_here], outs, (w_count, w_count, 2, 3, 3), cid,
                [((slots, toks, width), slot_err.dtype), (acts_here.shape, acts_here.dtype)])


def gather_pre_grad(pg, cid):
    w_count, r_count = lax.axis_size("wid"), lax.axis_size("rep")
    _, toks, columns = pg.shape

    def body(p_ref, o_ref, ssem, rsem, lsem, held):
        w, r = lax.axis_index("wid"), lax.axis_index("rep")
        barrier = pltpu.get_barrier_semaphore()

        def peers(step):
            others(w, w_count, lambda v: loop(0, r_count, lambda q: step(v, q)))
            others(r, r_count, lambda q: step(w, q))

        peers(lambda v, q: signal(barrier, wid=v, rep=q))
        pl.semaphore_wait(barrier, w_count * r_count - 1)

        def send(v, q):
            return remote(p_ref.at[q], o_ref.at[r, w], ssem.at[q * w_count + v],
                          rsem.at[r * w_count + w], wid=v, rep=q)

        def arrival(v, q):
            return remote(p_ref.at[q], o_ref.at[q, v], ssem.at[q * w_count + v],
                          rsem.at[q * w_count + v], wid=v, rep=q)

        peers(lambda v, q: send(v, q).start())
        own = bounce(p_ref.at[r], o_ref.at[r, w], held, lsem.at[0])
        peers(lambda v, q: arrival(v, q).wait_recv())
        peers(lambda v, q: send(v, q).wait_send())
        own.wait()

    out = jax.ShapeDtypeStruct((r_count, w_count, toks, columns), pg.dtype)
    total = w_count * r_count
    return comm(
        body, [pg], [out], (total, total, 1), cid, [((toks, columns), pg.dtype)]
    )[0]


def group_of(slots):
    return 3 if slots % 3 == 0 else 1


def slot_call(body, tables, args, in_specs, out_shape, out_spec, scratch, flops, name, grid):
    moved = sum(a.size * a.dtype.itemsize for a in args) + out_shape.size * out_shape.dtype.itemsize
    return pl.pallas_call(
        body,
        out_shape=out_shape,
        grid_spec=pltpu.PrefetchScalarGridSpec(
            num_scalar_prefetch=len(tables), grid=(grid,), in_specs=in_specs,
            out_specs=out_spec, scratch_shapes=scratch,
        ),
        compiler_params=pltpu.CompilerParams(vmem_limit_bytes=62 * 1024 * 1024),
        cost_estimate=pl.CostEstimate(flops=flops, bytes_accessed=moved, transcendentals=0),
        name=name,
    )(*tables, *args)


def decode(ids, tgt, valid, lat, dec_weight, layers):
    slots, block, width = dec_weight.shape
    blocks, toks, _ = lat.shape
    g = group_of(slots)

    def body(i_ref, t_ref, v_ref, lat_ref, w_ref, o_ref, acc):
        step = pl.program_id(0)

        @pl.when(step == 0)
        def _():
            acc[...] = jnp.zeros_like(acc)

        for i in range(g):
            k = step * g + i

            @pl.when(v_ref[k] > 0)
            def _():
                acc[t_ref[k]] += jnp.dot(
                    lat_ref[i_ref[k]], w_ref[i], preferred_element_type=F32
                )

        @pl.when(step == slots // g - 1)
        def _():
            o_ref[...] = acc[...].astype(o_ref.dtype)

    return slot_call(
        body, (ids, tgt, valid), (lat, dec_weight),
        [pl.BlockSpec((blocks, toks, block), lambda k, i, t, v: (0, 0, 0)),
         pl.BlockSpec((g, block, width), lambda k, i, t, v: (k, 0, 0))],
        jax.ShapeDtypeStruct((layers, toks, width), BF16),
        pl.BlockSpec((layers, toks, width), lambda k, i, t, v: (0, 0, 0)),
        [pltpu.VMEM((layers, toks, width), F32)], 2 * slots * toks * block * width, "decode",
        slots // g,
    )


def slot_errors(tgt, err, dec_weight):
    slots, block, width = dec_weight.shape
    layers, toks, _ = err.shape
    g = group_of(slots)

    def body(t_ref, e_ref, w_ref, o_ref):
        for i in range(g):
            k = pl.program_id(0) * g + i
            o_ref[i] = lax.dot_general(
                e_ref[t_ref[k]], w_ref[i], (((1,), (1,)), ((), ())), preferred_element_type=F32
            ).astype(o_ref.dtype)

    return slot_call(
        body, (tgt,), (err, dec_weight),
        [pl.BlockSpec((layers, toks, width), lambda k, t: (0, 0, 0)),
         pl.BlockSpec((g, block, width), lambda k, t: (k, 0, 0))],
        jax.ShapeDtypeStruct((slots, toks, block), BF16),
        pl.BlockSpec((g, toks, block), lambda k, t: (k, 0, 0)),
        [], 2 * slots * toks * block * width, "slot_errors", slots // g,
    )


def combine(ids, valid, parts, blocks_total):
    w_count, slots, toks, block = parts.shape

    g = slots // 3 if slots % 3 == 0 else 1

    def body(i_ref, v_ref, p_ref, o_ref, acc):
        step = pl.program_id(0)

        @pl.when(step == 0)
        def _():
            acc[...] = jnp.zeros_like(acc)

        for i in range(g):
            k = step * g + i

            @pl.when(v_ref[k] > 0)
            def _():
                acc[i_ref[k]] += jnp.sum(p_ref[:, i].astype(F32), axis=0)

        @pl.when(step == slots // g - 1)
        def _():
            o_ref[...] = acc[...].astype(o_ref.dtype)

    return slot_call(
        body, (ids, valid), (parts,),
        [pl.BlockSpec((w_count, g, toks, block), lambda k, i, v: (0, k, 0, 0))],
        jax.ShapeDtypeStruct((blocks_total, toks, block), BF16),
        pl.BlockSpec((blocks_total, toks, block), lambda k, i, v: (0, 0, 0)),
        [pltpu.VMEM((blocks_total, toks, block), F32)], w_count * slots * toks * block, "combine",
        slots // g,
    )


def decoder_grads(ids, tgt, valid, rep, lat, lat_twin, err, err_twin, slots):
    layers, toks, width = err.shape
    blocks, _, half = lat_twin.shape
    g = group_of(slots)

    def body(i_ref, t_ref, v_ref, r_ref, l_ref, lt_ref, e_ref, et_ref, o_ref):
        over = (((0,), (0,)), ((), ()))
        for i in range(g):
            k = pl.program_id(0) * g + i

            @pl.when(v_ref[k] > 0)
            def _():
                t, b = t_ref[k], i_ref[k]
                o_ref[i] = lax.dot_general(
                    l_ref[b], e_ref[t], over, preferred_element_type=F32
                ) + lax.dot_general(lt_ref[b], et_ref[t], over, preferred_element_type=F32)

            @pl.when(v_ref[k] == 0)
            def _():
                o_ref[i] = jnp.zeros_like(o_ref[i])

    return slot_call(
        body, (ids, tgt, valid, rep), (lat, lat_twin, err, err_twin),
        [pl.BlockSpec((blocks, toks, half), lambda k, i, t, v, r: (0, 0, r[0])),
         pl.BlockSpec((blocks, toks, half), lambda k, i, t, v, r: (0, 0, 0)),
         pl.BlockSpec((layers, toks, width), lambda k, i, t, v, r: (0, 0, 0)),
         pl.BlockSpec((layers, toks, width), lambda k, i, t, v, r: (0, 0, 0))],
        jax.ShapeDtypeStruct((slots, half, width), F32),
        pl.BlockSpec((g, half, width), lambda k, i, t, v, r: (k, 0, 0)),
        [], 4 * slots * toks * half * width, "decoder_grads", slots // g,
    )


def local(acts, targets, enc_weight, enc_bias, gate_mask, dec_list, dec_weight):
    layers, tok_rows, width_part = acts.shape
    lat_dev = enc_weight.shape[1]
    slots, block, _ = dec_weight.shape
    per_dev = lat_dev // block
    n, w_count, r_count = lax.axis_size("lay"), lax.axis_size("wid"), lax.axis_size("rep")
    lay, wid, rep = lax.axis_index("lay"), lax.axis_index("wid"), lax.axis_index("rep")
    lat_total = lat_dev * n
    blocks_total = lat_total // block
    latents_layer = lat_total // layers
    blocks_layer = latents_layer // block
    toks = tok_rows // w_count
    rows = tok_rows // n

    tgt = dec_list[:, 1]
    valid = (tgt >= 0).astype(jnp.int32)
    ids = jnp.maximum(dec_list[:, 0] * blocks_layer + dec_list[:, 2], 0)
    tgt = jnp.maximum(tgt, 0)

    here = lax.dynamic_index_in_dim(acts, lay * lat_dev // latents_layer, 0, keepdims=False)
    partial = jnp.dot(here, enc_weight, preferred_element_type=F32).astype(BF16)
    parts = exchange(
        "wid", partial.reshape(w_count, toks, lat_dev), (w_count, toks, lat_dev), (toks, lat_dev),
        lambda x, j: x.at[j], lambda o, j: o.at[j], 0,
    )
    shifted = jnp.sum(parts.astype(F32), axis=0) + enc_bias[None, :]
    shifted = shifted.reshape(toks, per_dev, block).transpose(1, 0, 2)
    keep = lax.dynamic_slice_in_dim(gate_mask, wid * toks, toks, 0).astype(F32).T[:, :, None]
    latent = (smooth_gate(shifted) * keep).astype(BF16)
    lat = gather_latents(latent, 1).reshape(blocks_total, tok_rows, block)

    recon_part = decode(ids, tgt, valid, lat, dec_weight, layers)
    recon_in = exchange(
        "lay", recon_part.reshape(layers, n, rows, width_part), (n, layers, rows, width_part),
        (layers, rows, width_part), lambda x, j: x.at[:, j], lambda o, j: o.at[j], 2,
    )
    recon = jnp.sum(recon_in.astype(F32), axis=0)
    own_target = lax.dynamic_slice_in_dim(targets, lay * rows, rows, 1)
    scale = float(tok_rows * r_count) ** (-0.5)
    own_err = ((recon - own_target.astype(F32)) * scale).astype(BF16)
    err = gather_errors(own_err, 3).reshape(layers, tok_rows, width_part)

    slot_err = slot_errors(tgt, err, dec_weight).reshape(slots, w_count, toks, block)
    slot_in, lat_twin, err_twin, acts_all = slots_and_twin(slot_err, lat, err, here, 4)
    outgoing = combine(ids, valid, slot_in, blocks_total)
    outgoing = outgoing.reshape(n, per_dev, toks, block)
    incoming = [lax.dynamic_index_in_dim(outgoing, lay, 0, keepdims=False)]
    for d in range(1, n):
        part = lax.dynamic_index_in_dim(outgoing, lax.rem(lay + d, n), 0, keepdims=False)
        incoming.append(lax.ppermute(part, "lay", [(i, (i + d) % n) for i in range(n)]))
    dec_out = decoder_grads(
        ids, tgt, valid, rep.reshape(1).astype(jnp.int32), lat, lat_twin, err, err_twin, slots
    )
    latent_error = sum(part.astype(F32) for part in incoming)
    pre_grad = (latent_error * keep * gate_slope(shifted)).astype(BF16)
    columns = lat_dev // r_count
    pre_grad = pre_grad.transpose(1, 0, 2).reshape(toks, r_count, columns).transpose(1, 0, 2)
    pre_all = gather_pre_grad(pre_grad, 6).reshape(r_count, tok_rows, columns)

    enc_out = lax.dot_general(
        acts_all.reshape(r_count * tok_rows, width_part),
        pre_all.reshape(r_count * tok_rows, columns), (((0,), (0,)), ((), ())),
        preferred_element_type=F32,
    )
    bias_out = jnp.sum(pre_all.astype(F32), axis=(0, 1))
    return (enc_out, bias_out, dec_out)


def solution(mesh):
    return jax.shard_map(
        local,
        mesh=mesh,
        in_specs=(
            P(None, ("grp", "rep"), "wid"),
            P(None, ("grp", "rep"), "wid"),
            P("wid", "lay"),
            P("lay"),
            P(("grp", "rep"), "lay"),
            P("lay", None),
            P("lay", None, "wid"),
        ),
        out_specs=(
            P(("grp", "wid"), ("lay", "rep")),
            P(("grp", "lay", "rep")),
            P(("grp", "lay"), "rep", "wid"),
        ),
        check_vma=False,
    )
```

profile of v0, /device:TPU:0, one launch (start us, length us, event | category | flops | bytes accessed | tf_op | source)
XLA Modules:
  0.0 300.3 jit_solution(18126379484798321967)
XLA Ops:
  0.6 1.4 maximum_bitcast_fusion
  2.0 1.3 fusion.11.v_ref
  4.4 4.6 %convolution_convert_fusion = bf16[256,2048]{1,0:T(8,128)(2,1)} fusion(bf16[256,1024]{1,0:T(8,128)(2,1)S(1)} %dynamic-slice_bitcast_fusion.3.a_ref, bf16[1024,2048]{1,0:T(8,128)(2,1)} %param.9), kind=kOutput, calls=%fused_computation.1 | convolution fusion | flops 1074266112 | bytes 5767168 | tf_op jit(solution)/shard_map/dot_general | solution.py:459
  9.0 15.2 %exchange_0.1 = bf16[2,128,2048]{2,1,0:T(8,128)(2,1)} custom-call(bf16[2,128,2048]{2,1,0:T(8,128)(2,1)} %bitcast.68), custom_call_target="tpu_custom_call" | custom-call | tf_op jit(solution)/shard_map/exchange_0/pallas_call | solution.py:107
  24.2 1.5 convert_reduce_fusion.2
  25.8 1.3 copy.13
  27.1 1.6 copy.14
  28.7 1.2 multiply_convert_fusion.1.h_ref
  29.9 50.6 %exchange_1.1 = bf16[32,2,128,256]{3,2,1,0:T(8,128)(2,1)} custom-call(bf16[8,128,256]{2,1,0:T(8,128)(2,1)} %multiply_convert_fusion.1.h_ref), custom_call_target="tpu_custom_call" | custom-call | tf_op jit(solution)/shard_map/exchange_1/pallas_call | solution.py:107
  80.5 13.1 %decode.1 = bf16[4,256,1024]{2,1,0:T(8,128)(2,1)} custom-call(s32[21]{0:T(128)} %get-tuple-element.14.i_ref, s32[21]{0:T(128)} %get-tuple-element.15.t_ref, s32[21]{0:T(128)} %fusion.11.v_ref, bf16[32,256,256]{2,1,0:T(8,128)(2,1)} %bitcast.53, bf16[21,256,1024]{2,1,0:T(8,128)(2,1)} %w_ref.3), custom_call_target="tpu_custom_call" | custom-call | flops 2818572288 | bytes 17301504 | tf_op jit(solution)/shard_map/decode/pallas_call | solution.py:302
  93.6 36.0 %exchange_2.1 = bf16[4,4,64,1024]{3,2,1,0:T(8,128)(2,1)} custom-call(bf16[4,4,64,1024]{3,2,1,0:T(8,128)(2,1)} %bitcast.63), custom_call_target="tpu_custom_call" | custom-call | tf_op jit(solution)/shard_map/exchange_2/pallas_call | solution.py:107
  129.5 2.1 convert_reduce_fusion
  131.6 2.0 multiply_convert_fusion.e_ref
  133.6 46.4 %exchange_3.1 = bf16[4,4,64,1024]{3,2,1,0:T(8,128)(2,1)} custom-call(bf16[4,64,1024]{2,1,0:T(8,128)(2,1)} %multiply_convert_fusion.e_ref), custom_call_target="tpu_custom_call" | custom-call | tf_op jit(solution)/shard_map/exchange_3/pallas_call | solution.py:107
  180.0 10.7 %slot_errors.1 = bf16[21,256,256]{2,1,0:T(8,128)(2,1)} custom-call(s32[21]{0:T(128)} %get-tuple-element.15.t_ref, bf16[4,256,1024]{2,1,0:T(8,128)(2,1)} %bitcast.56, bf16[21,256,1024]{2,1,0:T(8,128)(2,1)} %w_ref.3), custom_call_target="tpu_custom_call" | custom-call | flops 2818572288 | bytes 15859712 | tf_op jit(solution)/shard_map/slot_errors/pallas_call | solution.py:302
  190.7 31.8 %exchange_4.1 = (bf16[2,21,128,256]{3,2,1,0:T(8,128)(2,1)}, bf16[32,256,128]{2,1,0:T(8,128)(2,1)}, bf16[4,256,1024]{2,1,0:T(8,128)(2,1)}, bf16[2,256,1024]{2,1,0:T(8,128)(2,1)}) custom-call(bf16[21,2,128,256]{3,2,1,0:T(8,128)(2,1)} %bitcast.59, bf16[32,256,256]{2,1,0:T(8,128)(2,1)} %bitcast.54, bf16[4,256,1024]{2,1,0:T(8,128)(2,1)} %bitcast.57, ...), custom_call_target="tpu_custom_call" | custom-call | tf_op jit(solution)/shard_map/exchange_4/pallas_call | solution.py:107
  222.5 5.2 %combine.1 = bf16[32,128,256]{2,1,0:T(8,128)(2,1)} custom-call(s32[21]{0:T(128)} %get-tuple-element.14.i_ref, s32[21]{0:T(128)} %fusion.11.v_ref, bf16[2,21,128,256]{3,2,1,0:T(8,128)(2,1)} %get-tuple-element.8.p_ref), custom_call_target="tpu_custom_call" | custom-call | flops 1376256 | bytes 4849664 | tf_op jit(solution)/shard_map/combine/pallas_call | solution.py:302
  227.7 2.5 dynamic-slice_bitcast_fusion.2
  232.3 12.8 %decoder_grads.1 = f32[21,128,1024]{2,1,0:T(8,128)} custom-call(s32[21]{0:T(128)} %get-tuple-element.14.i_ref, s32[21]{0:T(128)} %get-tuple-element.15.t_ref, s32[21]{0:T(128)} %fusion.11.v_ref, s32[1]{0:T(128)} %bitcast.22.r_ref, bf16[32,256,256]{2,1,0:T(8,128)(2,1)} %bitcast.55, bf16[32,256,128]{2,1,0:T(8,128)(2,1)} %get-tuple-element.9.lt_ref, ...), custom_call_target="tpu_custom_call" | custom-call | flops 2818572288 | bytes 21495808 | tf_op jit(solution)/shard_map/decoder_grads/pallas_call | solution.py:302
  245.1 30.4 %collective-permute-done.1 = bf16[8,128,256]{2,1,0:T(8,128)(2,1)} collective-permute-done((bf16[8,128,256]{2,1,0:T(8,128)(2,1)}, bf16[8,128,256]{2,1,0:T(8,128)(2,1)}, u32[]{:S(2)}, u32[]{:S(2)}) %collective-permute-start.1) | collective-permute-done | bytes 524320 | tf_op jit(solution)/shard_map/ppermute | solution.py:488
  275.5 2.3 fusion.10
  279.1 14.6 %exchange_6.1 = bf16[2,2,128,1024]{3,2,1,0:T(8,128)(2,1)} custom-call(bf16[2,128,1024]{2,1,0:T(8,128)(2,1)} %bitcast.65), custom_call_target="tpu_custom_call" | custom-call | tf_op jit(solution)/shard_map/exchange_6/pallas_call | solution.py:107
  293.7 2.0 convert_reduce_fusion.1
  295.7 4.5 %fusion.12 = f32[1024,1024]{1,0:T(8,128)} fusion(bf16[512,1024]{1,0:T(8,128)(2,1)S(1)} %bitcast.67, bf16[512,1024]{1,0:T(8,128)(2,1)} %bitcast.60), kind=kOutput, calls=%fused_computation.30 | convolution fusion | flops 1073741824 | bytes 6291456 | tf_op jit(solution)/shard_map/dot_general | solution.py:498
  (18 shorter events, 4.4 us)
Async XLA Ops:
  4.4 4.6 %copy-start = (bf16[256,1024]{1,0:T(8,128)(2,1)}, bf16[256,1024]{1,0:T(8,128)(2,1)S(1)}, u32[]{:S(2)}) copy-start(bf16[256,1024]{1,0:T(8,128)(2,1)S(1)} %dynamic-slice_bitcast_fusion.3.a_ref) | copy-start | bytes 1572868
  25.8 2.9 copy-start.2
  25.8 2.9 copy-start.3
  230.2 14.9 %collective-permute-start.2 = (bf16[8,128,256]{2,1,0:T(8,128)(2,1)}, bf16[8,128,256]{2,1,0:T(8,128)(2,1)S(1)}, u32[]{:S(2)}, u32[]{:S(2)}) collective-permute-start(bf16[8,128,256]{2,1,0:T(8,128)(2,1)} %get-tuple-element.12), channel_id=1, source_target_pairs={{0,12},{4,0},{8,4},{12,8},{1,13},{5,1},{9,5},{13,9},{2,14},{6,2},{... | collective-permute-start | bytes 1572872 | tf_op jit(solution)/shard_map/ppermute | solution.py:488
  231.4 44.1 %collective-permute-start.1 = (bf16[8,128,256]{2,1,0:T(8,128)(2,1)}, bf16[8,128,256]{2,1,0:T(8,128)(2,1)}, u32[]{:S(2)}, u32[]{:S(2)}) collective-permute-start(bf16[8,128,256]{2,1,0:T(8,128)(2,1)} %get-tuple-element.13), channel_id=1, source_target_pairs={{0,8},{4,12},{8,0},{12,4},{1,9},{5,13},{9,1},{13,5},{2,10},{6,14},... | collective-permute-start | bytes 1572872 | tf_op jit(solution)/shard_map/ppermute | solution.py:488
  231.4 44.1 %collective-permute-start = (bf16[8,128,256]{2,1,0:T(8,128)(2,1)}, bf16[8,128,256]{2,1,0:T(8,128)(2,1)}, u32[]{:S(2)}, u32[]{:S(2)}) collective-permute-start(bf16[8,128,256]{2,1,0:T(8,128)(2,1)} %get-tuple-element.11), channel_id=1, source_target_pairs={{0,4},{4,8},{8,12},{12,0},{1,5},{5,9},{9,13},{13,1},{2,6},{6,10},{... | collective-permute-start | bytes 1572872 | tf_op jit(solution)/shard_map/ppermute | solution.py:488
  278.1 17.6 %copy-start.1 = (bf16[2,256,1024]{2,1,0:T(8,128)(2,1)S(1)}, bf16[2,256,1024]{2,1,0:T(8,128)(2,1)}, u32[]{:S(2)}) copy-start(bf16[2,256,1024]{2,1,0:T(8,128)(2,1)} %get-tuple-element.7) | copy-start | bytes 3145732
where the time goes:
time: 302 us; the launch traced here: 300 us
  Pallas kernels  236 us (78%)
  waiting for transfers between devices  30.4 us (10%)
  other arithmetic  13.8 us (5%)
  matrix products  9.13 us (3%)
  local copies, waits for them, and re-layouts  7.79 us (3%)
    pallas_call x6, Pallas kernels, comm(): pl.pallas_call(body, out_shape=tuple(outs), in_specs=[ANY] * len(args), o...  195 us
    pallas_call x4, Pallas kernels, slot_call(): pl.pallas_call(body, out_shape=out_shape, grid_spec=pltpu.PrefetchScalarG...  41.8 us
    ppermute x3, waiting for transfers between devices, local(): lax.ppermute(part, 'lay', [(i, (i + d) % n) for i in range(n)])  30.4 us
  transfers between devices with their start and end apart: 3, of which 1 were waited for; matrix products, arithmetic and copies ran while one was open for 0% of the time, Pallas kernels for 4%

commit v1 on v0

--- a/solution.py
+++ b/solution.py
@@ -10,6 +10,8 @@
 MESH = pl.DeviceIdType.MESH
 BF16 = jnp.bfloat16
 F32 = jnp.float32
+CUTS = 2
+SKEW = 3
 
 
 def smooth_gate(shifted):
@@ -144,26 +146,6 @@
         body, [x], [jax.ShapeDtypeStruct(out_shape, x.dtype)], (n, n, 1), cid,
         [(held_shape, x.dtype)],
     )[0]
-
-
-def gather_errors(e, cid):
-    n = lax.axis_size("lay")
-
-    def body(e_ref, o_ref, zs, zr, lsem, held):
-        l = lax.axis_index("lay")
-        barrier = pltpu.get_barrier_semaphore()
-        others(l, n, lambda j: signal(barrier, lay=j))
-        pl.semaphore_wait(barrier, n - 1)
-        take, finish = line_gather(
-            l, n, e_ref, lambda j: o_ref.at[:, j], zs, zr, lambda j: None
-        )
-        own = bounce(e_ref, o_ref.at[:, l], held, lsem.at[0])
-        take()
-        finish()
-        own.wait()
-
-    out = jax.ShapeDtypeStruct((e.shape[0], n) + e.shape[1:], e.dtype)
-    return comm(body, [e], [out], (n + 1, n, 1), cid, [(e.shape, e.dtype)])[0]
 
 
 def gather_latents(h, cid):
@@ -312,40 +294,224 @@
     )(*tables, *args)
 
 
-def decode(ids, tgt, valid, lat, dec_weight, layers):
-    slots, block, width = dec_weight.shape
-    blocks, toks, _ = lat.shape
-    g = group_of(slots)
-
-    def body(i_ref, t_ref, v_ref, lat_ref, w_ref, o_ref, acc):
-        step = pl.program_id(0)
-
-        @pl.when(step == 0)
-        def _():
-            acc[...] = jnp.zeros_like(acc)
-
-        for i in range(g):
-            k = step * g + i
-
-            @pl.when(v_ref[k] > 0)
-            def _():
-                acc[t_ref[k]] += jnp.dot(
-                    lat_ref[i_ref[k]], w_ref[i], preferred_element_type=F32
-                )
-
-        @pl.when(step == slots // g - 1)
-        def _():
-            o_ref[...] = acc[...].astype(o_ref.dtype)
-
-    return slot_call(
-        body, (ids, tgt, valid), (lat, dec_weight),
-        [pl.BlockSpec((blocks, toks, block), lambda k, i, t, v: (0, 0, 0)),
-         pl.BlockSpec((g, block, width), lambda k, i, t, v: (k, 0, 0))],
-        jax.ShapeDtypeStruct((layers, toks, width), BF16),
-        pl.BlockSpec((layers, toks, width), lambda k, i, t, v: (0, 0, 0)),
-        [pltpu.VMEM((layers, toks, width), F32)], 2 * slots * toks * block * width, "decode",
-        slots // g,
-    )
+class Tables:
+    def __init__(self, slots, layers, blocks):
+        self.tgt, self.id, self.valid = 0, slots, 2 * slots
+        self.prev_tgt, self.prev_id = 3 * slots, 4 * slots
+        self.last_tgt = 5 * slots
+        self.last_id = self.last_tgt + layers + 1
+        self.size = -(-(self.last_id + blocks + 1) // 128) * 128
+
+
+def slot_tables(dec_list, layers, blocks, blocks_layer):
+    slots = dec_list.shape[0]
+    at = Tables(slots, layers, blocks)
+
+    def body(d_ref, o_ref):
+        def clear(i, c):
+            o_ref[i] = 0
+            return c
+
+        lax.fori_loop(0, at.size, clear, 0)
+
+        def one(k, c):
+            s, t, b = d_ref[k, 0], d_ref[k, 1], d_ref[k, 2]
+            listed = t >= 0
+            group = jnp.where(listed, t, layers)
+            ident = jnp.where(listed, s * blocks_layer + b, blocks)
+            o_ref[at.tgt + k] = jnp.maximum(t, 0)
+            o_ref[at.id + k] = jnp.where(listed, ident, 0)
+            o_ref[at.valid + k] = jnp.where(listed, 1, 0)
+            o_ref[at.prev_tgt + k] = o_ref[at.last_tgt + group]
+            o_ref[at.last_tgt + group] = k + 1
+            o_ref[at.prev_id + k] = o_ref[at.last_id + ident]
+            o_ref[at.last_id + ident] = k + 1
+            return c
+
+        lax.fori_loop(0, slots, one, 0)
+
+    return pl.pallas_call(
+        body,
+        out_shape=jax.ShapeDtypeStruct((at.size,), jnp.int32),
+        in_specs=[pl.BlockSpec(memory_space=pltpu.SMEM)],
+        out_specs=pl.BlockSpec(memory_space=pltpu.SMEM),
+        name="slot_tables",
+    )(dec_list)
+
+
+def chunk_count(toks):
+    return next(c for c in (4, 2, 1) if toks % (16 * c) == 0 or c == 1)
+
+
+def decode_total(tables, lat, dec_weight, targets, scale, cid):
+    blocks, w_count, toks, block = lat.shape
+    slots, _, width = dec_weight.shape
+    layers = targets.shape[0]
+    n = lax.axis_size("lay")
+    at = Tables(slots, layers, blocks)
+    chunks = chunk_count(toks)
+    ct = toks // chunks
+    rows = w_count * ct
+    cuts = next(c for c in (CUTS, 1) if width % (128 * c) == 0)
+    part = width // cuts
+    steps = layers * cuts
+    pieces = chunks * steps
+    per_step = -(-slots // steps)
+
+    def body(tab, lat_ref, w_hbm, t_ref, e_ref, w_ref, sums, own, up_in, dn_in, up_out, dn_out,
+             wsem, us, ur, ds, dr):
+        l = lax.axis_index("lay")
+
+        def weight(k):
+            return pltpu.make_async_copy(w_hbm.at[k], w_ref.at[k], wsem.at[k])
+
+        loop(0, slots, lambda k: weight(k).start())
+        barrier = pltpu.get_barrier_semaphore()
+        others(l, n, lambda j: signal(barrier, lay=j))
+        sums[0] = jnp.zeros_like(sums[0])
+        pl.semaphore_wait(barrier, n - 1)
+
+        def slot(c, k):
+            held = lat_ref[tab[at.id + k], :, pl.ds(pl.multiple_of(c * ct, ct), ct), :]
+            made = jnp.dot(held.reshape(rows, block), w_ref[k], preferred_element_type=F32)
+            sums[k + 1] = made + sums[tab[at.prev_tgt + k]]
+
+        def emit(c):
+            for t in range(layers):
+                total = sums[tab[at.last_tgt + t]]
+                for i in range(cuts):
+                    own[(c * layers + t) * cuts + i] = total[:, i * part:(i + 1) * part]
+
+        def first(k, c):
+            weight(k).wait()
+            slot(0, k)
+            return c
+
+        lax.fori_loop(0, slots, first, 0)
+        emit(0)
+
+        def up(q):
+            return remote(up_out.at[q], up_in.at[q], us.at[q], ur.at[q], lay=l + 1)
+
+        def dn(q):
+            return remote(dn_out.at[q], dn_in.at[q], ds.at[q], dr.at[q], lay=l - 1)
+
+        def landed_up(q):
+            remote(up_in.at[q], up_in.at[q], us.at[q], ur.at[q], lay=l).wait_recv()
+
+        def landed_dn(q):
+            remote(dn_in.at[q], dn_in.at[q], ds.at[q], dr.at[q], lay=l).wait_recv()
+
+        def inside(q):
+            return (q >= 0) & (q < pieces)
+
+        def hand_on(s):
+            q, p = s - SKEW * l, s - SKEW * (n - 1 - l)
+
+            @pl.when(inside(q) & (l > 0))
+            def _():
+                landed_up(q)
+
+            @pl.when(inside(q) & (l == 0))
+            def _():
+                up_out[q] = own[q].astype(BF16)
+
+            @pl.when(inside(q) & (l > 0) & (l < n - 1))
+            def _():
+                up_out[q] = (own[q] + up_in[q].astype(F32)).astype(BF16)
+
+            @pl.when(inside(p) & (l < n - 1))
+            def _():
+                landed_dn(p)
+
+            @pl.when(inside(p) & (l == n - 1))
+            def _():
+                dn_out[p] = own[p].astype(BF16)
+
+            @pl.when(inside(p) & (l > 0) & (l < n - 1))
+            def _():
+                dn_out[p] = (own[p] + dn_in[p].astype(F32)).astype(BF16)
+
+            e = s - SKEW * jnp.maximum(l, n - 1 - l)
+
+            def error(total):
+                c, i = e // steps, lax.rem(e, steps)
+                t, i = i // cuts, lax.rem(i, cuts)
+                where = pl.ds(pl.multiple_of(c * ct, ct), ct)
+                over = pl.ds(pl.multiple_of(i * part, part), part)
+                aim = t_ref[t, :, where, over].reshape(rows, part).astype(F32)
+                e_ref[t, :, where, over] = ((total - aim) * scale).astype(BF16).reshape(w_count, ct, part)
+
+            @pl.when(inside(e) & (l == 0))
+            def _():
+                error(own[e] + dn_in[e].astype(F32))
+
+            @pl.when(inside(e) & (l == n - 1))
+            def _():
+                error(own[e] + up_in[e].astype(F32))
+
+            @pl.when(inside(e) & (l > 0) & (l < n - 1))
+            def _():
+                error(own[e] + up_in[e].astype(F32) + dn_in[e].astype(F32))
+
+            @pl.when(inside(q) & (l < n - 1))
+            def _():
+                up(q).start()
+
+            @pl.when(inside(p) & (l > 0))
+            def _():
+                dn(p).start()
+
+        def turn(s, carry):
+            hand_on(s)
+            c, i = s // steps + 1, lax.rem(s, steps)
+
+            @pl.when(c < chunks)
+            def _():
+                for j in range(per_step):
+                    @pl.when(i * per_step + j < slots)
+                    def _():
+                        slot(c, i * per_step + j)
+
+                @pl.when(i == steps - 1)
+                def _():
+                    emit(c)
+
+            return carry
+
+        lax.fori_loop(0, pieces + SKEW * (n - 1), turn, 0)
+
+        def sent(q, c):
+            @pl.when(l < n - 1)
+            def _():
+                up(q).wait_send()
+
+            @pl.when(l > 0)
+            def _():
+                dn(q).wait_send()
+
+            return c
+
+        lax.fori_loop(0, pieces, sent, 0)
+
+    piece = (pieces, rows, part)
+    vmem = pl.BlockSpec(memory_space=pltpu.VMEM)
+    return pl.pallas_call(
+        body,
+        out_shape=jax.ShapeDtypeStruct((layers, w_count, toks, width), BF16),
+        in_specs=[pl.BlockSpec(memory_space=pltpu.SMEM), vmem, ANY, vmem],
+        out_specs=vmem,
+        scratch_shapes=[
+            pltpu.VMEM(dec_weight.shape, dec_weight.dtype),
+            pltpu.VMEM((slots + 1, rows, width), F32),
+            pltpu.VMEM(piece, F32),
+        ] + [pltpu.VMEM(piece, BF16)] * 4 + [pltpu.SemaphoreType.DMA((slots,))]
+        + [pltpu.SemaphoreType.DMA((pieces,))] * 4,
+        compiler_params=pltpu.CompilerParams(
+            collective_id=cid, has_side_effects=True, vmem_limit_bytes=62 * 1024 * 1024
+        ),
+        name="decode_total",
+    )(tables, lat, dec_weight, targets)
 
 
 def slot_errors(tgt, err, dec_weight):
@@ -448,7 +614,6 @@
     latents_layer = lat_total // layers
     blocks_layer = latents_layer // block
     toks = tok_rows // w_count
-    rows = tok_rows // n
 
     tgt = dec_list[:, 1]
     valid = (tgt >= 0).astype(jnp.int32)
@@ -465,18 +630,14 @@
     shifted = shifted.reshape(toks, per_dev, block).transpose(1, 0, 2)
     keep = lax.dynamic_slice_in_dim(gate_mask, wid * toks, toks, 0).astype(F32).T[:, :, None]
     latent = (smooth_gate(shifted) * keep).astype(BF16)
-    lat = gather_latents(latent, 1).reshape(blocks_total, tok_rows, block)
-
-    recon_part = decode(ids, tgt, valid, lat, dec_weight, layers)
-    recon_in = exchange(
-        "lay", recon_part.reshape(layers, n, rows, width_part), (n, layers, rows, width_part),
-        (layers, rows, width_part), lambda x, j: x.at[:, j], lambda o, j: o.at[j], 2,
-    )
-    recon = jnp.sum(recon_in.astype(F32), axis=0)
-    own_target = lax.dynamic_slice_in_dim(targets, lay * rows, rows, 1)
+    lat = gather_latents(latent, 1)
+
     scale = float(tok_rows * r_count) ** (-0.5)
-    own_err = ((recon - own_target.astype(F32)) * scale).astype(BF16)
-    err = gather_errors(own_err, 3).reshape(layers, tok_rows, width_part)
+    err = decode_total(
+        slot_tables(dec_list, layers, blocks_total, blocks_layer), lat, dec_weight,
+        targets.reshape(layers, w_count, toks, width_part), scale, 2,
+    ).reshape(layers, tok_rows, width_part)
+    lat = lat.reshape(blocks_total, tok_rows, block)
 
     slot_err = slot_errors(tgt, err, dec_weight).reshape(slots, w_count, toks, block)
     slot_in, lat_twin, err_twin, acts_all = slots_and_twin(slot_err, lat, err, here, 4)

time: 302 us -> 272 us (0.901)
  Pallas kernels: 236 us -> 209 us
  other arithmetic: 13.8 us -> 9.59 us
    pallas_call x6 -> x4, Pallas kernels: 195 us -> 112 us  [comm(): pl.pallas_call(body, out_shape=tuple(outs), in_specs=[ANY] * len(args), o...]
    pallas_call x0 -> x2, Pallas kernels: none -> 68.6 us  [the longest x1 65.1 us: decode_total(): pl.pallas_call(body, out_shape=jax.ShapeDtypeStruct((layers, w_count, tok...]
    pallas_call x4 -> x3, Pallas kernels: 41.8 us -> 28.4 us  [slot_call(): pl.pallas_call(body, out_shape=out_shape, grid_spec=pltpu.PrefetchScalarG...]
  transfers between devices with their start and end apart: 3 -> 3, of which waited for: 1 -> 1; matrix products, arithmetic and copies ran while one was open for 0% -> 0% of each run, Pallas kernels for 4% -> 5%
where the time goes in v1:
time: 272 us; the launch traced here: 271 us
  Pallas kernels  209 us (77%)
  waiting for transfers between devices  30.7 us (11%)
  other arithmetic  9.59 us (4%)
  local copies, waits for them, and re-layouts  9.18 us (3%)
  matrix products  9.13 us (3%)
    pallas_call x4, Pallas kernels, comm(): pl.pallas_call(body, out_shape=tuple(outs), in_specs=[ANY] * len(args), o...  112 us
    pallas_call x1, Pallas kernels, decode_total(): pl.pallas_call(body, out_shape=jax.ShapeDtypeStruct((layers, w_count, tok...  65.1 us
    ppermute x3, waiting for transfers between devices, local(): lax.ppermute(part, 'lay', [(i, (i + d) % n) for i in range(n)])  30.7 us
    pallas_call x3, Pallas kernels, slot_call(): pl.pallas_call(body, out_shape=out_shape, grid_spec=pltpu.PrefetchScalarG...  28.4 us
  transfers between devices with their start and end apart: 3, of which 1 were waited for; matrix products, arithmetic and copies ran while one was open for 0% of the time, Pallas kernels for 5%

profile of v1, /device:TPU:0, one launch (start us, length us, event | category | flops | bytes accessed | tf_op | source)
XLA Modules:
  0.0 270.6 jit_solution(3246422197494007058)
XLA Ops:
  0.6 1.3 maximum_bitcast_fusion
  2.0 1.4 copy.15.d_ref
  3.3 1.2 fusion.11.v_ref
  4.5 3.4 %slot_tables.1.tab = s32[256]{0:T(256)} custom-call(s32[21,3]{1,0:T(8,128)} %copy.15.d_ref), custom_call_target="tpu_custom_call" | custom-call | tf_op jit(solution)/shard_map/slot_tables/pallas_call | solution.py:333
  8.0 1.1 dynamic-slice_bitcast_fusion.3.a_ref
  9.1 4.6 %convolution_convert_fusion = bf16[256,2048]{1,0:T(8,128)(2,1)} fusion(bf16[256,1024]{1,0:T(8,128)(2,1)S(1)} %dynamic-slice_bitcast_fusion.3.a_ref, bf16[1024,2048]{1,0:T(8,128)(2,1)} %param.9), kind=kOutput, calls=%fused_computation | convolution fusion | flops 1074266112 | bytes 5767168 | tf_op jit(solution)/shard_map/dot_general | solution.py:624
  13.7 15.3 %exchange_0.1 = bf16[2,128,2048]{2,1,0:T(8,128)(2,1)} custom-call(bf16[2,128,2048]{2,1,0:T(8,128)(2,1)} %bitcast.67), custom_call_target="tpu_custom_call" | custom-call | tf_op jit(solution)/shard_map/exchange_0/pallas_call | solution.py:109
  28.9 1.5 convert_reduce_fusion.1
  30.5 1.3 copy.16
  31.8 1.6 copy.17
  33.4 1.2 multiply_convert_fusion.h_ref
  34.6 50.6 %exchange_1.1.lat_ref = bf16[32,2,128,256]{3,2,1,0:T(8,128)(2,1)} custom-call(bf16[8,128,256]{2,1,0:T(8,128)(2,1)} %multiply_convert_fusion.h_ref), custom_call_target="tpu_custom_call" | custom-call | tf_op jit(solution)/shard_map/exchange_1/pallas_call | solution.py:109
  85.2 65.1 %decode_total.1 = bf16[4,2,128,1024]{3,2,1,0:T(8,128)(2,1)} custom-call(s32[256]{0:T(256)} %slot_tables.1.tab, bf16[32,2,128,256]{3,2,1,0:T(8,128)(2,1)} %exchange_1.1.lat_ref, bf16[21,256,1024]{2,1,0:T(8,128)(2,1)} %w_ref.1, bf16[4,2,128,1024]{3,2,1,0:T(8,128)(2,1)} %bitcast.63), custom_call_target="tpu_custom_call" | custom-call | tf_op jit(solution)/shard_map/decode_total/pallas_call | solution.py:499
  150.3 10.7 %slot_errors.1 = bf16[21,256,256]{2,1,0:T(8,128)(2,1)} custom-call(s32[21]{0:T(128)} %get-tuple-element.15.t_ref, bf16[4,256,1024]{2,1,0:T(8,128)(2,1)} %bitcast.55, bf16[21,256,1024]{2,1,0:T(8,128)(2,1)} %w_ref.1), custom_call_target="tpu_custom_call" | custom-call | flops 2818572288 | bytes 15859712 | tf_op jit(solution)/shard_map/slot_errors/pallas_call | solution.py:284
  161.0 31.7 %exchange_4.1 = (bf16[2,21,128,256]{3,2,1,0:T(8,128)(2,1)}, bf16[32,256,128]{2,1,0:T(8,128)(2,1)}, bf16[4,256,1024]{2,1,0:T(8,128)(2,1)}, bf16[2,256,1024]{2,1,0:T(8,128)(2,1)}) custom-call(bf16[21,2,128,256]{3,2,1,0:T(8,128)(2,1)} %bitcast.58, bf16[32,256,256]{2,1,0:T(8,128)(2,1)} %bitcast.53, bf16[4,256,1024]{2,1,0:T(8,128)(2,1)} %bitcast.56, ...), custom_call_target="tpu_custom_call" | custom-call | tf_op jit(solution)/shard_map/exchange_4/pallas_call | solution.py:109
  192.7 5.2 %combine.1 = bf16[32,128,256]{2,1,0:T(8,128)(2,1)} custom-call(s32[21]{0:T(128)} %get-tuple-element.14.i_ref, s32[21]{0:T(128)} %fusion.11.v_ref, bf16[2,21,128,256]{3,2,1,0:T(8,128)(2,1)} %get-tuple-element.8.p_ref), custom_call_target="tpu_custom_call" | custom-call | flops 1376256 | bytes 4849664 | tf_op jit(solution)/shard_map/combine/pallas_call | solution.py:284
  197.9 2.6 dynamic-slice_bitcast_fusion.2
  200.5 1.5 collective-permute-start.2
  202.6 12.5 %decoder_grads.1 = f32[21,128,1024]{2,1,0:T(8,128)} custom-call(s32[21]{0:T(128)} %get-tuple-element.14.i_ref, s32[21]{0:T(128)} %get-tuple-element.15.t_ref, s32[21]{0:T(128)} %fusion.11.v_ref, s32[1]{0:T(128)} %bitcast.22.r_ref, bf16[32,256,256]{2,1,0:T(8,128)(2,1)} %bitcast.54, bf16[32,256,128]{2,1,0:T(8,128)(2,1)} %get-tuple-element.9.lt_ref, ...), custom_call_target="tpu_custom_call" | custom-call | flops 2818572288 | bytes 21495808 | tf_op jit(solution)/shard_map/decoder_grads/pallas_call | solution.py:284
  215.1 30.7 %collective-permute-done.1 = bf16[8,128,256]{2,1,0:T(8,128)(2,1)} collective-permute-done((bf16[8,128,256]{2,1,0:T(8,128)(2,1)}, bf16[8,128,256]{2,1,0:T(8,128)(2,1)}, u32[]{:S(2)}, u32[]{:S(2)}) %collective-permute-start.1) | collective-permute-done | bytes 524320 | tf_op jit(solution)/shard_map/ppermute | solution.py:649
  245.8 2.3 fusion.10
  249.4 14.6 %exchange_6.1 = bf16[2,2,128,1024]{3,2,1,0:T(8,128)(2,1)} custom-call(bf16[2,128,1024]{2,1,0:T(8,128)(2,1)} %bitcast.64), custom_call_target="tpu_custom_call" | custom-call | tf_op jit(solution)/shard_map/exchange_6/pallas_call | solution.py:109
  264.0 2.0 convert_reduce_fusion
  266.0 4.5 %fusion.12 = f32[1024,1024]{1,0:T(8,128)} fusion(bf16[512,1024]{1,0:T(8,128)(2,1)S(1)} %bitcast.66, bf16[512,1024]{1,0:T(8,128)(2,1)} %bitcast.59), kind=kOutput, calls=%fused_computation.28 | convolution fusion | flops 1073741824 | bytes 6291456 | tf_op jit(solution)/shard_map/dot_general | solution.py:659
  (16 shorter events, 1.9 us)
Async XLA Ops:
  9.1 4.6 %copy-start = (bf16[256,1024]{1,0:T(8,128)(2,1)}, bf16[256,1024]{1,0:T(8,128)(2,1)S(1)}, u32[]{:S(2)}) copy-start(bf16[256,1024]{1,0:T(8,128)(2,1)S(1)} %dynamic-slice_bitcast_fusion.3.a_ref) | copy-start | bytes 1572868
  30.4 2.9 %copy-start.2 = (f32[2048]{0:T(1024)S(1)}, f32[2048]{0:T(1024)}, u32[]{:S(2)}) copy-start(f32[2048]{0:T(1024)} %param.10) | copy-start | bytes 24580
  30.5 2.9 %copy-start.3 = (s32[256,8]{0,1:T(8,128)S(1)}, s32[256,8]{0,1:T(8,128)}, u32[]{:S(2)}) copy-start(s32[256,8]{0,1:T(8,128)} %param.11) | copy-start | bytes 24580
  200.5 14.6 %collective-permute-start.2 = (bf16[8,128,256]{2,1,0:T(8,128)(2,1)}, bf16[8,128,256]{2,1,0:T(8,128)(2,1)S(1)}, u32[]{:S(2)}, u32[]{:S(2)}) collective-permute-start(bf16[8,128,256]{2,1,0:T(8,128)(2,1)} %get-tuple-element.12), channel_id=1, source_target_pairs={{0,12},{4,0},{8,4},{12,8},{1,13},{5,1},{9,5},{13,9},{2,14},{6,2},{... | collective-permute-start | bytes 1572872 | tf_op jit(solution)/shard_map/ppermute | solution.py:649
  202.0 43.8 %collective-permute-start.1 = (bf16[8,128,256]{2,1,0:T(8,128)(2,1)}, bf16[8,128,256]{2,1,0:T(8,128)(2,1)}, u32[]{:S(2)}, u32[]{:S(2)}) collective-permute-start(bf16[8,128,256]{2,1,0:T(8,128)(2,1)} %get-tuple-element.13), channel_id=1, source_target_pairs={{0,8},{4,12},{8,0},{12,4},{1,9},{5,13},{9,1},{13,5},{2,10},{6,14},... | collective-permute-start | bytes 1572872 | tf_op jit(solution)/shard_map/ppermute | solution.py:649
  202.0 43.8 %collective-permute-start = (bf16[8,128,256]{2,1,0:T(8,128)(2,1)}, bf16[8,128,256]{2,1,0:T(8,128)(2,1)}, u32[]{:S(2)}, u32[]{:S(2)}) collective-permute-start(bf16[8,128,256]{2,1,0:T(8,128)(2,1)} %get-tuple-element.11), channel_id=1, source_target_pairs={{0,4},{4,8},{8,12},{12,0},{1,5},{5,9},{9,13},{13,1},{2,6},{6,10},{... | collective-permute-start | bytes 1572872 | tf_op jit(solution)/shard_map/ppermute | solution.py:649
  248.4 17.6 %copy-start.1 = (bf16[2,256,1024]{2,1,0:T(8,128)(2,1)S(1)}, bf16[2,256,1024]{2,1,0:T(8,128)(2,1)}, u32[]{:S(2)}) copy-start(bf16[2,256,1024]{2,1,0:T(8,128)(2,1)} %get-tuple-element.7) | copy-start | bytes 3145732

commit v2 on v1

--- a/solution.py
+++ b/solution.py
@@ -12,6 +12,7 @@
 F32 = jnp.float32
 CUTS = 2
 SKEW = 3
+Z_SKEW = 3
 
 
 def smooth_gate(shifted):
@@ -187,91 +188,6 @@
     out = jax.ShapeDtypeStruct((n * blocks, w_count, toks, width), h.dtype)
     return comm(
         body, [h], [out], (n + 1, n, n * w_count, n * w_count, 1), cid, [(h.shape, h.dtype)]
-    )[0]
-
-
-def slots_and_twin(slot_err, lat, err, acts_here, cid):
-    w_count, r_count = lax.axis_size("wid"), lax.axis_size("rep")
-    assert r_count == 2
-    slots, _, toks, width = slot_err.shape
-    half = width // r_count
-
-    def body(s_ref, l_ref, e_ref, a_ref, so_ref, lo_ref, eo_ref, ao_ref, ssem, rsem, lsem, ts, tr,
-             held, held_acts):
-        w, r = lax.axis_index("wid"), lax.axis_index("rep")
-        twin = 1 - r
-        barrier = pltpu.get_barrier_semaphore()
-        others(w, w_count, lambda v: signal(barrier, wid=v))
-        signal(barrier, rep=twin)
-        pl.semaphore_wait(barrier, w_count)
-
-        def send(v):
-            return remote(s_ref.at[:, v], so_ref.at[w], ssem.at[v], rsem.at[w], wid=v)
-
-        def arrival(v):
-            return remote(s_ref.at[:, w], so_ref.at[v], ssem.at[v], rsem.at[v], wid=v)
-
-        others(w, w_count, lambda v: send(v).start())
-        twins = [
-            remote(l_ref.at[:, :, pl.ds(pl.multiple_of(twin * half, half), half)], lo_ref,
-                   ts.at[0], tr.at[0], rep=twin),
-            remote(e_ref, eo_ref, ts.at[1], tr.at[1], rep=twin),
-            remote(a_ref, ao_ref.at[r], ts.at[2], tr.at[2], rep=twin),
-        ]
-        for c in twins:
-            c.start()
-        own = bounce(s_ref.at[:, w], so_ref.at[w], held, lsem.at[0])
-        own_acts = bounce(a_ref, ao_ref.at[r], held_acts, lsem.at[1])
-        others(w, w_count, lambda v: arrival(v).wait_recv())
-        others(w, w_count, lambda v: send(v).wait_send())
-        own.wait()
-        own_acts.wait()
-        for c in twins:
-            c.wait()
-
-    outs = [
-        jax.ShapeDtypeStruct((w_count, slots, toks, width), slot_err.dtype),
-        jax.ShapeDtypeStruct(lat.shape[:2] + (half,), lat.dtype),
-        jax.ShapeDtypeStruct(err.shape, err.dtype),
-        jax.ShapeDtypeStruct((r_count,) + acts_here.shape, acts_here.dtype),
-    ]
-    return comm(body, [slot_err, lat, err, acts_here], outs, (w_count, w_count, 2, 3, 3), cid,
-                [((slots, toks, width), slot_err.dtype), (acts_here.shape, acts_here.dtype)])
-
-
-def gather_pre_grad(pg, cid):
-    w_count, r_count = lax.axis_size("wid"), lax.axis_size("rep")
-    _, toks, columns = pg.shape
-
-    def body(p_ref, o_ref, ssem, rsem, lsem, held):
-        w, r = lax.axis_index("wid"), lax.axis_index("rep")
-        barrier = pltpu.get_barrier_semaphore()
-
-        def peers(step):
-            others(w, w_count, lambda v: loop(0, r_count, lambda q: step(v, q)))
-            others(r, r_count, lambda q: step(w, q))
-
-        peers(lambda v, q: signal(barrier, wid=v, rep=q))
-        pl.semaphore_wait(barrier, w_count * r_count - 1)
-
-        def send(v, q):
-            return remote(p_ref.at[q], o_ref.at[r, w], ssem.at[q * w_count + v],
-                          rsem.at[r * w_count + w], wid=v, rep=q)
-
-        def arrival(v, q):
-            return remote(p_ref.at[q], o_ref.at[q, v], ssem.at[q * w_count + v],
-                          rsem.at[q * w_count + v], wid=v, rep=q)
-
-        peers(lambda v, q: send(v, q).start())
-        own = bounce(p_ref.at[r], o_ref.at[r, w], held, lsem.at[0])
-        peers(lambda v, q: arrival(v, q).wait_recv())
-        peers(lambda v, q: send(v, q).wait_send())
-        own.wait()
-
-    out = jax.ShapeDtypeStruct((r_count, w_count, toks, columns), pg.dtype)
-    total = w_count * r_count
-    return comm(
-        body, [pg], [out], (total, total, 1), cid, [((toks, columns), pg.dtype)]
     )[0]
 
 
@@ -514,59 +430,304 @@
     )(tables, lat, dec_weight, targets)
 
 
-def slot_errors(tgt, err, dec_weight):
-    slots, block, width = dec_weight.shape
-    layers, toks, _ = err.shape
+def latent_errors(tables, err, dec_weight, slope, lat, acts_here, cid):
+    layers, w_count, toks, width = err.shape
+    slots, block, _ = dec_weight.shape
+    per_dev = slope.shape[0]
+    n, r_count = lax.axis_size("lay"), lax.axis_size("rep")
+    assert r_count == 2
+    blocks = lat.shape[0]
+    columns = per_dev * block // r_count
+    at = Tables(slots, layers, blocks)
+    chunks = chunk_count(toks)
+    ct = toks // chunks
+    rows = w_count * ct
+    split = 2 if per_dev % 2 == 0 else 1
+    pb = per_dev // split
+    steps = (n - 1) * split
+    pieces = chunks * steps
     g = group_of(slots)
-
-    def body(t_ref, e_ref, w_ref, o_ref):
-        for i in range(g):
-            k = pl.program_id(0) * g + i
-            o_ref[i] = lax.dot_general(
-                e_ref[t_ref[k]], w_ref[i], (((1,), (1,)), ((), ())), preferred_element_type=F32
-            ).astype(o_ref.dtype)
-
-    return slot_call(
-        body, (tgt,), (err, dec_weight),
-        [pl.BlockSpec((layers, toks, width), lambda k, t: (0, 0, 0)),
-         pl.BlockSpec((g, block, width), lambda k, t: (k, 0, 0))],
-        jax.ShapeDtypeStruct((slots, toks, block), BF16),
-        pl.BlockSpec((g, toks, block), lambda k, t: (k, 0, 0)),
-        [], 2 * slots * toks * block * width, "slot_errors", slots // g,
-    )
-
-
-def combine(ids, valid, parts, blocks_total):
-    w_count, slots, toks, block = parts.shape
-
-    g = slots // 3 if slots % 3 == 0 else 1
-
-    def body(i_ref, v_ref, p_ref, o_ref, acc):
-        step = pl.program_id(0)
-
-        @pl.when(step == 0)
-        def _():
-            acc[...] = jnp.zeros_like(acc)
-
-        for i in range(g):
-            k = step * g + i
-
-            @pl.when(v_ref[k] > 0)
-            def _():
-                acc[i_ref[k]] += jnp.sum(p_ref[:, i].astype(F32), axis=0)
-
-        @pl.when(step == slots // g - 1)
-        def _():
-            o_ref[...] = acc[...].astype(o_ref.dtype)
-
-    return slot_call(
-        body, (ids, valid), (parts,),
-        [pl.BlockSpec((w_count, g, toks, block), lambda k, i, v: (0, k, 0, 0))],
-        jax.ShapeDtypeStruct((blocks_total, toks, block), BF16),
-        pl.BlockSpec((blocks_total, toks, block), lambda k, i, v: (0, 0, 0)),
-        [pltpu.VMEM((blocks_total, toks, block), F32)], w_count * slots * toks * block, "combine",
-        slots // g,
-    )
+    groups = slots // g
+    lead = min(2, chunks)
+    half = block // r_count
+
+    def body(tab, e_ref, w_hbm, sl_ref, l_ref, a_ref, po_ref, lo_ref, eo_ref, ao_ref,
+             w_ref, x_out, x_in, sums, made, up_in, dn_in, up_out, dn_out, twin_out,
+             wsem, xs, xr, us, ur, ds, dr, ts, tr, ps, pr, asem):
+        l, w, r = lax.axis_index("lay"), lax.axis_index("wid"), lax.axis_index("rep")
+        twin = 1 - r
+
+        def weight(k):
+            return pltpu.make_async_copy(w_hbm.at[k], w_ref.at[k], wsem.at[k])
+
+        loop(0, slots, lambda k: weight(k).start())
+        barrier = pltpu.get_barrier_semaphore()
+        others(l, n, lambda j: signal(barrier, lay=j))
+        others(w, w_count, lambda v: signal(barrier, wid=v))
+        signal(barrier, rep=twin)
+        sums[0] = jnp.zeros_like(sums[0])
+        pl.semaphore_wait(barrier, n + w_count - 1)
+
+        def chunk(c):
+            return pl.ds(pl.multiple_of(c * ct, ct), ct)
+
+        def x_send(c, i, v):
+            where = pl.ds(i * g, g)
+            return remote(x_out.at[c, v, where], x_in.at[c, w, where], xs.at[(c * groups + i) * w_count + v],
+                          xr.at[(c * groups + i) * w_count + w], wid=v)
+
+        def x_landed(c, i, v):
+            where = pl.ds(i * g, g)
+            return remote(x_in.at[c, v, where], x_in.at[c, v, where],
+                          xs.at[(c * groups + i) * w_count + v],
+                          xr.at[(c * groups + i) * w_count + v], wid=v)
+
+        def slot_group(c, i, fresh=False):
+            for k in [i * g + d for d in range(g)]:
+                if fresh:
+                    weight(k).wait()
+                held = e_ref[tab[at.tgt + k], :, chunk(c), :].reshape(rows, width)
+                part = lax.dot_general(
+                    held, w_ref[k], (((1,), (1,)), ((), ())), preferred_element_type=F32
+                ).astype(BF16).reshape(w_count, ct, block)
+                for v in range(w_count):
+                    x_out[c, v, k] = part[v]
+            others(w, w_count, lambda v: x_send(c, i, v).start())
+
+        twins = [
+            remote(l_ref.at[:, :, :, pl.ds(pl.multiple_of(twin * half, half), half)], lo_ref,
+                   ts.at[0], tr.at[0], rep=twin),
+            remote(e_ref, eo_ref, ts.at[1], tr.at[1], rep=twin),
+        ] + [
+            remote(a_ref.at[v], ao_ref.at[lax.rem(v - w + w_count, w_count), r], ts.at[2 + v], tr.at[2 + v],
+                   rep=twin)
+            for v in range(w_count)
+        ]
+        mine = [
+            pltpu.make_async_copy(
+                a_ref.at[v], ao_ref.at[lax.rem(v - w + w_count, w_count), r], asem.at[v])
+            for v in range(w_count)
+        ]
+
+        def gather(c):
+            def landed(i, carry):
+                others(w, w_count, lambda v: x_landed(c, i, v).wait_recv())
+                return carry
+
+            lax.fori_loop(0, groups, landed, 0)
+
+            def one(k, carry):
+                total = sums[tab[at.prev_id + k]] + x_out[c, w, k].astype(F32)
+                for d in range(1, w_count):
+                    total = total + x_in[c, lax.rem(w + d, w_count), k].astype(F32)
+                sums[k + 1] = total
+                return carry
+
+            lax.fori_loop(0, slots, one, 0)
+
+            def out(b, carry):
+                made[c, b] = sums[tab[at.last_id + b]]
+                return carry
+
+            lax.fori_loop(0, blocks, out, 0)
+
+        lax.fori_loop(0, groups, lambda i, z: (slot_group(0, i, True), z)[1], 0)
+        for c in range(1, lead):
+            lax.fori_loop(0, groups, lambda i, z: (slot_group(c, i), z)[1], 0)
+        for c in twins + mine:
+            c.start()
+        gather(0)
+
+        def up(q):
+            return remote(up_out.at[q], up_in.at[q], us.at[q], ur.at[q], lay=l + 1)
+
+        def dn(q):
+            return remote(dn_out.at[q], dn_in.at[q], ds.at[q], dr.at[q], lay=l - 1)
+
+        def landed_up(q):
+            remote(up_in.at[q], up_in.at[q], us.at[q], ur.at[q], lay=l).wait_recv()
+
+        def landed_dn(q):
+            remote(dn_in.at[q], dn_in.at[q], ds.at[q], dr.at[q], lay=l).wait_recv()
+
+        def inside(q):
+            return (q >= 0) & (q < pieces)
+
+        def own(q, dest):
+            return made[q // steps, pl.ds(dest * per_dev + lax.rem(q, split) * pb, pb)]
+
+        def tick(s, carry):
+            q, p = s - Z_SKEW * l, s - Z_SKEW * (n - 1 - l)
+            to_up = n - 1 - lax.rem(q + steps, steps) // split
+            to_dn = lax.rem(p + steps, steps) // split
+
+            @pl.when(inside(q) & (l > 0) & (to_up >= l))
+            def _():
+                landed_up(q)
+
+            @pl.when(inside(q) & (l == 0))
+            def _():
+                up_out[q] = own(q, to_up).astype(BF16)
+
+            @pl.when(inside(q) & (l > 0) & (to_up > l))
+            def _():
+                up_out[q] = (own(q, to_up) + up_in[q].astype(F32)).astype(BF16)
+
+            @pl.when(inside(p) & (l < n - 1) & (to_dn <= l))
+            def _():
+                landed_dn(p)
+
+            @pl.when(inside(p) & (l == n - 1))
+            def _():
+                dn_out[p] = own(p, to_dn).astype(BF16)
+
+            @pl.when(inside(p) & (l < n - 1) & (to_dn < l))
+            def _():
+                dn_out[p] = (own(p, to_dn) + dn_in[p].astype(F32)).astype(BF16)
+
+            off_up = (n - 1 - l) * split
+            off_dn = l * split
+            f = s - jnp.maximum(off_up + Z_SKEW * l, off_dn + Z_SKEW * (n - 1 - l))
+            c, i = f // steps, lax.rem(f + steps, steps)
+            whole = inside(f) & (i < split)
+
+            def finish(total):
+                blocks_here = pl.ds(i * pb, pb)
+                grad = (total * sl_ref[blocks_here, chunk(c), :]).astype(BF16)
+                if split == r_count:
+                    @pl.when(i == r)
+                    def _():
+                        for b in range(pb):
+                            po_ref[r, chunk(c), b * block:(b + 1) * block] = grad[b]
+
+                    @pl.when(i != r)
+                    def _():
+                        for b in range(pb):
+                            twin_out[c, :, b * block:(b + 1) * block] = grad[b]
+                else:
+                    for b in range(pb):
+                        for side in range(r_count):
+                            part = grad[b][:, side * half:(side + 1) * half]
+
+                            @pl.when(r == side)
+                            def _():
+                                po_ref[side, chunk(c), b * half:(b + 1) * half] = part
+
+                            @pl.when(r != side)
+                            def _():
+                                twin_out[c, :, b * half:(b + 1) * half] = part
+
+            def mid():
+                return made[c, pl.ds(l * per_dev + i * pb, pb)]
+
+            @pl.when(whole & (l == 0))
+            def _():
+                finish(mid() + dn_in[c * steps + off_dn + i].astype(F32))
+
+            @pl.when(whole & (l == n - 1))
+            def _():
+                finish(mid() + up_in[c * steps + off_up + i].astype(F32))
+
+            @pl.when(whole & (l > 0) & (l < n - 1))
+            def _():
+                finish(mid() + up_in[c * steps + off_up + i].astype(F32)
+                       + dn_in[c * steps + off_dn + i].astype(F32))
+
+            @pl.when(inside(q) & (to_up > l))
+            def _():
+                up(q).start()
+
+            @pl.when(inside(p) & (to_dn < l))
+            def _():
+                dn(p).start()
+
+            @pl.when(whole & (i == split - 1))
+            def _():
+                twin_pre(c).start()
+
+            c, i = s // steps, lax.rem(s, steps)
+
+            @pl.when(c + lead < chunks)
+            def _():
+                lax.fori_loop(
+                    (i * groups + steps - 1) // steps, ((i + 1) * groups + steps - 1) // steps,
+                    lambda j, z: (slot_group(c + lead, j), z)[1], 0,
+                )
+
+            @pl.when((c + 1 < chunks) & (i == steps - 1))
+            def _():
+                gather(c + 1)
+
+            return carry
+
+        def twin_pre(c):
+            return remote(twin_out.at[c], po_ref.at[r, chunk(c)], ps.at[c], pr.at[c], rep=twin)
+
+        def twin_landed(c):
+            return remote(twin_out.at[c], po_ref.at[twin, chunk(c)], ps.at[c], pr.at[c], rep=twin)
+
+        lax.fori_loop(0, (chunks - 1) * steps + split + (n - 1) * max(split, Z_SKEW), tick, 0)
+
+        def sent(q, carry):
+            to_up = n - 1 - lax.rem(q, steps) // split
+            to_dn = lax.rem(q, steps) // split
+
+            @pl.when(to_up > l)
+            def _():
+                up(q).wait_send()
+
+            @pl.when(to_dn < l)
+            def _():
+                dn(q).wait_send()
+
+            return carry
+
+        lax.fori_loop(0, pieces, sent, 0)
+
+        def x_sent(q, carry):
+            others(w, w_count, lambda v: x_send(q // groups, lax.rem(q, groups), v).wait_send())
+            return carry
+
+        lax.fori_loop(0, chunks * groups, x_sent, 0)
+        for c in range(chunks):
+            twin_landed(c).wait()
+        for c in twins:
+            c.wait()
+        for c in mine:
+            c.wait()
+
+    piece = (pieces, pb, ct, block)
+    x_shape = (chunks, w_count, slots, ct, block)
+    vmem = pl.BlockSpec(memory_space=pltpu.VMEM)
+    x_sems = chunks * groups * w_count
+    dma = pltpu.SemaphoreType.DMA
+    return pl.pallas_call(
+        body,
+        out_shape=(
+            jax.ShapeDtypeStruct((r_count, toks, columns), BF16),
+            jax.ShapeDtypeStruct(lat.shape[:3] + (half,), lat.dtype),
+            jax.ShapeDtypeStruct(err.shape, err.dtype),
+            jax.ShapeDtypeStruct((w_count, r_count, toks, width), acts_here.dtype),
+        ),
+        in_specs=[pl.BlockSpec(memory_space=pltpu.SMEM), vmem, ANY, vmem, ANY, vmem],
+        out_specs=(vmem, ANY, ANY, ANY),
+        scratch_shapes=[
+            pltpu.VMEM(dec_weight.shape, dec_weight.dtype),
+            pltpu.VMEM(x_shape, BF16),
+            pltpu.VMEM(x_shape, BF16),
+            pltpu.VMEM((slots + 1, ct, block), F32),
+            pltpu.VMEM((chunks, blocks, ct, block), F32),
+        ] + [pltpu.VMEM(piece, BF16)] * 4 + [
+            pltpu.VMEM((chunks, ct, columns), BF16),
+            dma((slots,)), dma((x_sems,)), dma((x_sems,)),
+        ] + [dma((pieces,))] * 4 + [
+            dma((2 + w_count,)), dma((2 + w_count,)), dma((chunks,)), dma((chunks,)), dma((w_count,)),
+        ],
+        compiler_params=pltpu.CompilerParams(
+            collective_id=cid, has_side_effects=True, vmem_limit_bytes=62 * 1024 * 1024
+        ),
+        name="latent_errors",
+    )(tables, err, dec_weight, slope, lat, acts_here)
 
 
 def decoder_grads(ids, tgt, valid, rep, lat, lat_twin, err, err_twin, slots):
@@ -633,35 +794,31 @@
     lat = gather_latents(latent, 1)
 
     scale = float(tok_rows * r_count) ** (-0.5)
+    tables = slot_tables(dec_list, layers, blocks_total, blocks_layer)
     err = decode_total(
-        slot_tables(dec_list, layers, blocks_total, blocks_layer), lat, dec_weight,
-        targets.reshape(layers, w_count, toks, width_part), scale, 2,
-    ).reshape(layers, tok_rows, width_part)
-    lat = lat.reshape(blocks_total, tok_rows, block)
-
-    slot_err = slot_errors(tgt, err, dec_weight).reshape(slots, w_count, toks, block)
-    slot_in, lat_twin, err_twin, acts_all = slots_and_twin(slot_err, lat, err, here, 4)
-    outgoing = combine(ids, valid, slot_in, blocks_total)
-    outgoing = outgoing.reshape(n, per_dev, toks, block)
-    incoming = [lax.dynamic_index_in_dim(outgoing, lay, 0, keepdims=False)]
-    for d in range(1, n):
-        part = lax.dynamic_index_in_dim(outgoing, lax.rem(lay + d, n), 0, keepdims=False)
-        incoming.append(lax.ppermute(part, "lay", [(i, (i + d) % n) for i in range(n)]))
+        tables, lat, dec_weight, targets.reshape(layers, w_count, toks, width_part), scale, 2
+    )
+    slope = gate_slope(shifted) * keep
+    pre_mine, lat_twin, err_twin, acts_all = latent_errors(
+        tables, err, dec_weight, slope, lat, here.reshape(w_count, toks, width_part), 3
+    )
+    pre_all = [pre_mine] + [
+        lax.ppermute(pre_mine, "wid", [(i, (i - d) % w_count) for i in range(w_count)])
+        for d in range(1, w_count)
+    ]
+    half = block // r_count
     dec_out = decoder_grads(
-        ids, tgt, valid, rep.reshape(1).astype(jnp.int32), lat, lat_twin, err, err_twin, slots
+        ids, tgt, valid, rep.reshape(1).astype(jnp.int32),
+        lat.reshape(blocks_total, tok_rows, block), lat_twin.reshape(blocks_total, tok_rows, half),
+        err.reshape(layers, tok_rows, width_part), err_twin.reshape(layers, tok_rows, width_part), slots,
     )
-    latent_error = sum(part.astype(F32) for part in incoming)
-    pre_grad = (latent_error * keep * gate_slope(shifted)).astype(BF16)
     columns = lat_dev // r_count
-    pre_grad = pre_grad.transpose(1, 0, 2).reshape(toks, r_count, columns).transpose(1, 0, 2)
-    pre_all = gather_pre_grad(pre_grad, 6).reshape(r_count, tok_rows, columns)
-
+    pre_all = jnp.stack(pre_all).reshape(r_count * tok_rows, columns)
     enc_out = lax.dot_general(
-        acts_all.reshape(r_count * tok_rows, width_part),
-        pre_all.reshape(r_count * tok_rows, columns), (((0,), (0,)), ((), ())),
+        acts_all.reshape(r_count * tok_rows, width_part), pre_all, (((0,), (0,)), ((), ())),
         preferred_element_type=F32,
     )
-    bias_out = jnp.sum(pre_all.astype(F32), axis=(0, 1))
+    bias_out = jnp.sum(pre_all.astype(F32), axis=0)
     return (enc_out, bias_out, dec_out)
 
 

time: 272 us -> 226 us (0.83)
  waiting for transfers between devices: 30.7 us -> 0.01 us
  local copies, waits for them, and re-layouts: 9.18 us -> 3.82 us
  other arithmetic: 9.59 us -> 5.28 us
  Pallas kernels: 209 us -> 205 us
    pallas_call x0 -> x1, Pallas kernels: none -> 58.2 us  [latent_errors(): pl.pallas_call(body, out_shape=(jax.ShapeDtypeStruct((r_count, toks, colu...]
    pallas_call x4 -> x2, Pallas kernels: 112 us -> 65.8 us  [comm(): pl.pallas_call(body, out_shape=tuple(outs), in_specs=[ANY] * len(args), o...]
    ppermute x3 -> x1, waiting for transfers between devices: 30.7 us -> 0.01 us  [local(): lax.ppermute(pre_mine, 'wid', [(i, (i - d) % w_count) for i in range(w_co...]
    pallas_call x3 -> x1, Pallas kernels: 28.4 us -> 12.9 us  [slot_call(): pl.pallas_call(body, out_shape=out_shape, grid_spec=pltpu.PrefetchScalarG...]
    squeeze x2 -> x0, local copies, waits for them, and re-layouts: 3.65 us -> none  [the longest x1 2.57 us: local(): lax.dynamic_index_in_dim(outgoing, lax.rem(lay + d, n), 0, keepdims=False)]
  transfers between devices with their start and end apart: 3 -> 1, of which waited for: 1 -> 0; matrix products, arithmetic and copies ran while one was open for 0% -> 0% of each run, Pallas kernels for 5% -> 6%
where the time goes in v2:
time: 226 us; the launch traced here: 225 us
  Pallas kernels  205 us (91%)
  matrix products  9.13 us (4%)
  other arithmetic  5.28 us (2%)
  local copies, waits for them, and re-layouts  3.82 us (2%)
    pallas_call x2, Pallas kernels, comm(): pl.pallas_call(body, out_shape=tuple(outs), in_specs=[ANY] * len(args), o...  65.8 us
    pallas_call x1, Pallas kernels, decode_total(): pl.pallas_call(body, out_shape=jax.ShapeDtypeStruct((layers, w_count, tok...  65.1 us
    pallas_call x1, Pallas kernels, latent_errors(): pl.pallas_call(body, out_shape=(jax.ShapeDtypeStruct((r_count, toks, colu...  58.2 us
    pallas_call x1, Pallas kernels, slot_call(): pl.pallas_call(body, out_shape=out_shape, grid_spec=pltpu.PrefetchScalarG...  12.9 us
    dot_general x1, matrix products, local(): partial = jnp.dot(here, enc_weight, preferred_element_type=F32).astype(BF16)  4.6 us
    dot_general x1, matrix products, local(): lax.dot_general(acts_all.reshape(r_count * tok_rows, width_part), pre_all...  4.53 us
  transfers between devices with their start and end apart: 1, of which 0 were waited for; matrix products, arithmetic and copies ran while one was open for 0% of the time, Pallas kernels for 6%

profile of v2, /device:TPU:0, one launch (start us, length us, event | category | flops | bytes accessed | tf_op | source)
XLA Modules:
  0.0 224.9 jit_solution(12518900938648765149)
XLA Ops:
  0.7 0.7 add.38
  1.4 1.4 copy.15.d_ref
  2.7 3.4 %slot_tables.1.tab = s32[256]{0:T(256)} custom-call(s32[21,3]{1,0:T(8,128)} %copy.15.d_ref), custom_call_target="tpu_custom_call" | custom-call | tf_op jit(solution)/shard_map/slot_tables/pallas_call | solution.py:249
  6.2 1.1 constant_dynamic-slice_fusion
  7.2 0.0 copy-start.1
  7.2 4.6 %convolution_convert_fusion = bf16[256,2048]{1,0:T(8,128)(2,1)} fusion(bf16[1024,2048]{1,0:T(8,128)(2,1)} %param.9, bf16[1,256,1024]{2,1,0:T(8,128)(2,1)S(1)} %constant_dynamic-slice_fusion), kind=kOutput, calls=%fused_computation | convolution fusion | flops 1074266112 | bytes 5767168 | tf_op jit(solution)/shard_map/dot_general | solution.py:785
  11.9 15.3 %exchange_0.1 = bf16[2,128,2048]{2,1,0:T(8,128)(2,1)} custom-call(bf16[2,128,2048]{2,1,0:T(8,128)(2,1)} %bitcast.51), custom_call_target="tpu_custom_call" | custom-call | tf_op jit(solution)/shard_map/exchange_0/pallas_call | solution.py:110
  27.1 0.0 copy-done.1
  27.1 1.5 convert_reduce_fusion.1
  28.6 0.3 copy.16
  29.0 0.3 copy.17
  29.3 0.0 copy-done.3
  29.3 1.9 fusion.5
  31.3 50.6 %exchange_1.1.lat_ref.l_ref = bf16[32,2,128,256]{3,2,1,0:T(8,128)(2,1)} custom-call(bf16[8,128,256]{2,1,0:T(8,128)(2,1)} %get-tuple-element.12.h_ref), custom_call_target="tpu_custom_call" | custom-call | tf_op jit(solution)/shard_map/exchange_1/pallas_call | solution.py:110
  81.8 65.1 %decode_total.1.e_ref = bf16[4,2,128,1024]{3,2,1,0:T(8,128)(2,1)} custom-call(s32[256]{0:T(256)} %slot_tables.1.tab, bf16[32,2,128,256]{3,2,1,0:T(8,128)(2,1)} %exchange_1.1.lat_ref.l_ref, bf16[21,256,1024]{2,1,0:T(8,128)(2,1)} %w_hbm.3, bf16[4,2,128,1024]{3,2,1,0:T(8,128)(2,1)} %bitcast.43), custom_call_target="tpu_custom_call" | custom-call | tf_op jit(solution)/shard_map/decode_total/pallas_call | solution.py:415
  146.9 0.0 copy-start.2
  146.9 58.2 %latent_errors.1 = (bf16[2,128,1024]{2,1,0:T(8,128)(2,1)}, bf16[32,2,128,128]{3,2,1,0:T(8,128)(2,1)}, bf16[4,2,128,1024]{3,2,1,0:T(8,128)(2,1)}, bf16[2,2,128,1024]{3,2,1,0:T(8,128)(2,1)}) custom-call(s32[256]{0:T(256)} %slot_tables.1.tab, bf16[4,2,128,1024]{3,2,1,0:T(8,128)(2,1)} %decode_total.1.e_ref, bf16[21,256,1024]{2,1,0:T(8,128)(2,1)} %w_hbm.3, ...), custom_call_target="tpu_custom_call" | custom-call | tf_op jit(solution)/shard_map/latent_errors/pallas_call | solution.py:704
  205.1 0.5 collective-permute-start
  205.6 0.5 fusion.7.v_ref
  206.2 0.5 maximum_bitcast_fusion
  206.7 12.9 %decoder_grads.1 = f32[21,128,1024]{2,1,0:T(8,128)} custom-call(s32[21]{0:T(128)} %get-tuple-element.14.i_ref, s32[21]{0:T(128)} %get-tuple-element.13.t_ref, s32[21]{0:T(128)} %fusion.7.v_ref, s32[1]{0:T(128)} %bitcast.14.r_ref, bf16[32,256,256]{2,1,0:T(8,128)(2,1)} %bitcast.40, bf16[32,256,128]{2,1,0:T(8,128)(2,1)} %bitcast.49, ...), custom_call_target="tpu_custom_call" | custom-call | flops 2818572288 | bytes 21495808 | tf_op jit(solution)/shard_map/decoder_grads/pallas_call | solution.py:200
  219.6 0.0 collective-permute-done
  219.6 0.8 convert_reduce_fusion
  220.4 4.5 %convolution_bitcast_fusion = f32[1024,1024]{1,0:T(8,128)} fusion(bf16[2,2,128,1024]{3,2,1,0:T(8,128)(2,1)} %get-tuple-element.7, bf16[1,2,128,1024]{3,2,1,0:T(8,128)(2,1)S(1)} %bitcast.47, bf16[1,2,128,1024]{3,2,1,0:T(8,128)(2,1)S(1)} %bitcast.45), kind=kOutput, calls=%fused_computation.1 | convolution fusion | flops 1074266112 | bytes 6291456 | tf_op jit(solution)/shard_map/dot_general | solution.py:817
  (5 shorter events, 0.0 us)
Async XLA Ops:
  7.2 19.9 %copy-start.1 = (bf16[1,256,1024]{2,1,0:T(8,128)(2,1)}, bf16[1,256,1024]{2,1,0:T(8,128)(2,1)S(1)}, u32[]{:S(2)}) copy-start(bf16[1,256,1024]{2,1,0:T(8,128)(2,1)S(1)} %constant_dynamic-slice_fusion) | copy-start | bytes 1572868
  11.8 17.5 %copy-start.3 = (s32[256,8]{0,1:T(8,128)S(1)}, s32[256,8]{0,1:T(8,128)}, u32[]{:S(2)}) copy-start(s32[256,8]{0,1:T(8,128)} %param.11) | copy-start | bytes 24580
  146.9 58.8 %copy-start.2 = (s32[21,3]{0,1:T(4,128)S(1)}, s32[21,3]{0,1:T(4,128)}, u32[]{:S(2)}) copy-start(s32[21,3]{0,1:T(4,128)} %param.12) | copy-start | bytes 760
  205.1 14.5 %collective-permute-start = (bf16[2,128,1024]{2,1,0:T(8,128)(2,1)}, bf16[2,128,1024]{2,1,0:T(8,128)(2,1)S(1)}, u32[]{:S(2)}, u32[]{:S(2)}) collective-permute-start(bf16[2,128,1024]{2,1,0:T(8,128)(2,1)} %get-tuple-element.8), channel_id=1, source_target_pairs={{0,2},{2,0},{1,3},{3,1},{4,6},{6,4},{5,7},{7,5},{8,10},{10,8},{9,1... | collective-permute-start | bytes 1572872 | tf_op jit(solution)/shard_map/ppermute | solution.py:806
  206.7 12.9 %copy-start = (bf16[2,128,1024]{2,1,0:T(8,128)(2,1)S(1)}, bf16[2,128,1024]{2,1,0:T(8,128)(2,1)}, u32[]{:S(2)}) copy-start(bf16[2,128,1024]{2,1,0:T(8,128)(2,1)} %get-tuple-element.8) | copy-start | bytes 1572868

commit v3 on v2

v3 whole, which is shorter than its diff:
```python
import jax
import jax.numpy as jnp
from jax import lax
from jax.experimental import pallas as pl
from jax.experimental.pallas import tpu as pltpu
from jax.sharding import PartitionSpec as P

ROOT = 0.7978845608028654
CUBIC = 0.044715
MESH = pl.DeviceIdType.MESH
BF16 = jnp.bfloat16
F32 = jnp.float32
CUTS = 2
SKEW = 3
Z_SKEW = 3
A_GATE = 3
A_SKEW = 3
A_ACROSS = 3
C_ACROSS = 3


def smooth_gate(shifted):
    inside_arg = ROOT * (shifted + CUBIC * shifted * shifted * shifted)
    return 0.5 * shifted * (1.0 + jnp.tanh(inside_arg))


def gate_slope(shifted):
    inside_arg = ROOT * (shifted + CUBIC * shifted * shifted * shifted)
    tanh_part = jnp.tanh(inside_arg)
    return 0.5 * (1.0 + tanh_part) + 0.5 * shifted * (1.0 - tanh_part * tanh_part) * ROOT * (
        1.0 + 3.0 * CUBIC * shifted * shifted
    )


def loop(first, count, step):
    if count <= 4:
        for d in range(first, count):
            step(d)
    else:
        lax.fori_loop(first, count, lambda d, c: (step(d), c)[1], 0)


def others(me, count, step):
    loop(1, count, lambda d: step(lax.rem(me + d, count)))


def signal(barrier, **where):
    pl.semaphore_signal(barrier, inc=1, device_id=where, device_id_type=MESH)


def remote(src, dst, send_sem, recv_sem, **where):
    return pltpu.make_async_remote_copy(
        src_ref=src, dst_ref=dst, send_sem=send_sem, recv_sem=recv_sem, device_id=where,
        device_id_type=MESH,
    )


ANY = pl.BlockSpec(memory_space=pl.ANY)


def nearest(l, n, d, step):
    for j in (l - d, l + d):

        @pl.when((j >= 0) & (j < n))
        def _():
            step(j)


def group_of(slots):
    return 3 if slots % 3 == 0 else 1


def slot_call(body, tables, args, in_specs, out_shape, out_spec, scratch, flops, name, grid):
    moved = sum(a.size * a.dtype.itemsize for a in args) + out_shape.size * out_shape.dtype.itemsize
    return pl.pallas_call(
        body,
        out_shape=out_shape,
        grid_spec=pltpu.PrefetchScalarGridSpec(
            num_scalar_prefetch=len(tables), grid=(grid,), in_specs=in_specs,
            out_specs=out_spec, scratch_shapes=scratch,
        ),
        compiler_params=pltpu.CompilerParams(vmem_limit_bytes=62 * 1024 * 1024),
        cost_estimate=pl.CostEstimate(flops=flops, bytes_accessed=moved, transcendentals=0),
        name=name,
    )(*tables, *args)


class Tables:
    def __init__(self, slots, layers, blocks):
        self.tgt, self.id, self.valid = 0, slots, 2 * slots
        self.prev_tgt, self.prev_id = 3 * slots, 4 * slots
        self.last_tgt = 5 * slots
        self.last_id = self.last_tgt + layers + 1
        self.size = -(-(self.last_id + blocks + 1) // 128) * 128


def slot_tables(dec_list, layers, blocks, blocks_layer):
    slots = dec_list.shape[0]
    at = Tables(slots, layers, blocks)

    def body(d_ref, o_ref):
        def clear(i, c):
            o_ref[i] = 0
            return c

        lax.fori_loop(0, at.size, clear, 0)

        def one(k, c):
            s, t, b = d_ref[k, 0], d_ref[k, 1], d_ref[k, 2]
            listed = t >= 0
            group = jnp.where(listed, t, layers)
            ident = jnp.where(listed, s * blocks_layer + b, blocks)
            o_ref[at.tgt + k] = jnp.maximum(t, 0)
            o_ref[at.id + k] = jnp.where(listed, ident, 0)
            o_ref[at.valid + k] = jnp.where(listed, 1, 0)
            o_ref[at.prev_tgt + k] = o_ref[at.last_tgt + group]
            o_ref[at.last_tgt + group] = k + 1
            o_ref[at.prev_id + k] = o_ref[at.last_id + ident]
            o_ref[at.last_id + ident] = k + 1
            return c

        lax.fori_loop(0, slots, one, 0)

    return pl.pallas_call(
        body,
        out_shape=jax.ShapeDtypeStruct((at.size,), jnp.int32),
        in_specs=[pl.BlockSpec(memory_space=pltpu.SMEM)],
        out_specs=pl.BlockSpec(memory_space=pltpu.SMEM),
        name="slot_tables",
    )(dec_list)


def chunk_count(toks):
    return next(c for c in (4, 2, 1) if toks % (16 * c) == 0 or c == 1)


def step(tables, acts_here, enc_weight, enc_bias, gate, dec_weight, targets, scale, cid):
    w_count, toks, width = acts_here.shape
    lat_dev = enc_weight.shape[1]
    slots, block, _ = dec_weight.shape
    layers = targets.shape[0]
    per_dev = lat_dev // block
    n, r_count = lax.axis_size("lay"), lax.axis_size("rep")
    assert r_count == 2
    blocks = n * per_dev
    columns = lat_dev // r_count
    half = block // r_count
    at = Tables(slots, layers, blocks)
    chunks = chunk_count(toks)
    ct = toks // chunks
    rows = w_count * ct
    wide = min(lat_dev, 512)

    cuts = next(c for c in (CUTS, 1) if width % (128 * c) == 0)
    part = width // cuts
    b_steps = layers * cuts
    b_pieces = chunks * b_steps

    split = 2 if per_dev % 2 == 0 else 1
    pb = per_dev // split
    z_steps = (n - 1) * split
    z_pieces = chunks * z_steps
    g = group_of(slots)
    groups = slots // g

    period = max(b_steps, z_steps)
    per_step = -(-slots // period)
    a_decode = A_GATE + A_SKEW * (n - 1) + A_ACROSS
    b_first = a_decode + period
    c_slots = b_first + b_steps + SKEW * (n - 1)
    c_gather = c_slots + period + C_ACROSS
    ticks = c_gather + (chunks - 1) * period + split + (n - 1) * max(split, Z_SKEW)

    def body(tab, a_ref, ew_ref, b_ref, g_ref, w_hbm, t_ref,
             po_ref, lat_hbm, lo_ref, e_hbm, eo_ref, ao_ref,
             w_ref, lat_ref, lat_now, sl_ref, p_out, p_in, e_ref, sums, own_ref, bu_in, bd_in, bu_out, bd_out,
             x_out, x_in, c_sums, made, zu_in, zd_in, zu_out, zd_out, twin_out,
             wsem, ps, pr, aus, ads, azr, axs, axr, bus, bur, bds, bdr, xs, xr, zus, zur, zds, zdr,
             ts, tr, tps, tpr, asem):
        l, w, r = lax.axis_index("lay"), lax.axis_index("wid"), lax.axis_index("rep")
        twin = 1 - r

        def weight(k):
            return pltpu.make_async_copy(w_hbm.at[k], w_ref.at[k], wsem.at[k])

        loop(0, slots, lambda k: weight(k).start())
        barrier = pltpu.get_barrier_semaphore()
        others(l, n, lambda j: signal(barrier, lay=j))
        others(w, w_count, lambda v: signal(barrier, wid=v))
        signal(barrier, rep=twin)
        sums[0] = jnp.zeros_like(sums[0])
        c_sums[0] = jnp.zeros_like(c_sums[0])
        pl.semaphore_wait(barrier, n + w_count - 1)

        def chunk(c):
            return pl.ds(pl.multiple_of(c * ct, ct), ct)

        def at_chunk(s, first, do, last=0):
            t = s - first

            @pl.when((t >= 0) & (t < chunks * period))
            def _():
                @pl.when(lax.rem(t, period) == last)
                def _():
                    do(t // period)


        def p_send(c, v):
            return remote(p_out.at[c, v], p_in.at[c, w], ps.at[c * w_count + v], pr.at[c * w_count + w], wid=v)

        def p_landed(c, v):
            return remote(p_in.at[c, v], p_in.at[c, v], ps.at[c * w_count + v], pr.at[c * w_count + v], wid=v)

        def product(c):
            held = a_ref[:, chunk(c), :].reshape(rows, width)
            for o in range(0, lat_dev, wide):
                made_here = jnp.dot(held, ew_ref[:, o:o + wide], preferred_element_type=F32).astype(BF16)
                for v in range(w_count):
                    p_out[c, v, :, o:o + wide] = made_here[v * ct:(v + 1) * ct]
            others(w, w_count, lambda v: p_send(c, v).start())

        def shard(c, j, v):
            return lat_ref.at[pl.ds(j * per_dev, per_dev), v, chunk(c)]

        def a_up(c, j):
            return remote(shard(c, j, w), shard(c, j, w), aus.at[c * n + j], azr.at[c * n + j], lay=l + 1)

        def a_dn(c, j):
            return remote(shard(c, j, w), shard(c, j, w), ads.at[c * n + j], azr.at[c * n + j], lay=l - 1)

        def across(c, j, v, source):
            return remote(shard(c, j, source), shard(c, j, source), axs.at[(c * n + j) * w_count + v],
                          axr.at[(c * n + j) * w_count + source], wid=v)

        def goes(c, j, do):
            @pl.when((j <= l) & (l < n - 1))
            def _():
                do(a_up(c, j))

            @pl.when((j >= l) & (l > 0))
            def _():
                do(a_dn(c, j))

            others(w, w_count, lambda v: do(across(c, j, v, w)))

        def gated(c):
            others(w, w_count, lambda v: p_landed(c, v).wait_recv())
            keep = g_ref[w, chunk(c), :].astype(F32)
            for b in range(per_dev):
                over = slice(b * block, (b + 1) * block)
                shifted = p_out[c, w, :, over].astype(F32) + b_ref[:, over]
                for d in range(1, w_count):
                    shifted = shifted + p_in[c, lax.rem(w + d, w_count), :, over].astype(F32)
                held = keep[:, b:b + 1]
                lat_ref[l * per_dev + b, w, chunk(c), :] = (smooth_gate(shifted) * held).astype(BF16)
                sl_ref[b, chunk(c), :] = gate_slope(shifted) * held
            goes(c, l, lambda copy: copy.start())

        def take(c, j):
            remote(shard(c, j, w), shard(c, j, w), aus.at[c * n + j], azr.at[c * n + j], lay=j).wait_recv()
            goes(c, j, lambda copy: copy.start())

        def crossed(c):
            loop(0, n, lambda j: others(w, w_count, lambda v: across(c, j, v, v).wait_recv()))
            lat_now[...] = lat_ref[:, :, chunk(c), :]


        def slot(k):
            held = lat_now[tab[at.id + k]].reshape(rows, block)
            sums[k + 1] = jnp.dot(held, w_ref[k], preferred_element_type=F32) + sums[tab[at.prev_tgt + k]]

        def emit(c):
            for t in range(layers):
                total = sums[tab[at.last_tgt + t]].astype(BF16)
                for i in range(cuts):
                    own_ref[c * b_steps + t * cuts + i] = total[:, i * part:(i + 1) * part]

        def b_up(q):
            return remote(bu_out.at[q], bu_in.at[q], bus.at[q], bur.at[q], lay=l + 1)

        def b_dn(q):
            return remote(bd_out.at[q], bd_in.at[q], bds.at[q], bdr.at[q], lay=l - 1)

        def b_inside(q):
            return (q >= 0) & (q < chunks * period) & (lax.rem(q + period * chunks, period) < b_steps)

        def b_piece(q):
            return q // period * b_steps + lax.rem(q + period * chunks, period)

        def hand_on(s):
            q, p = s - SKEW * l, s - SKEW * (n - 1 - l)
            e = s - SKEW * jnp.maximum(l, n - 1 - l)
            q_in, p_in_, e_in = b_inside(q), b_inside(p), b_inside(e)
            q, p, e = b_piece(q), b_piece(p), b_piece(e)

            @pl.when(q_in & (l > 0))
            def _():
                remote(bu_in.at[q], bu_in.at[q], bus.at[q], bur.at[q], lay=l).wait_recv()

            @pl.when(q_in & (l == 0))
            def _():
                bu_out[q] = own_ref[q]

            @pl.when(q_in & (l > 0) & (l < n - 1))
            def _():
                bu_out[q] = (own_ref[q].astype(F32) + bu_in[q].astype(F32)).astype(BF16)

            @pl.when(p_in_ & (l < n - 1))
            def _():
                remote(bd_in.at[p], bd_in.at[p], bds.at[p], bdr.at[p], lay=l).wait_recv()

            @pl.when(p_in_ & (l == n - 1))
            def _():
                bd_out[p] = own_ref[p]

            @pl.when(p_in_ & (l > 0) & (l < n - 1))
            def _():
                bd_out[p] = (own_ref[p].astype(F32) + bd_in[p].astype(F32)).astype(BF16)

            def error(total):
                c, i = e // b_steps, lax.rem(e, b_steps)
                t, i = i // cuts, lax.rem(i, cuts)
                over = pl.ds(pl.multiple_of(i * part, part), part)
                aim = t_ref[t, :, chunk(c), over].reshape(rows, part).astype(F32)
                e_ref[t, :, chunk(c), over] = ((total - aim) * scale).astype(BF16).reshape(w_count, ct, part)

            @pl.when(e_in & (l == 0))
            def _():
                error(own_ref[e].astype(F32) + bd_in[e].astype(F32))

            @pl.when(e_in & (l == n - 1))
            def _():
                error(own_ref[e].astype(F32) + bu_in[e].astype(F32))

            @pl.when(e_in & (l > 0) & (l < n - 1))
            def _():
                error(own_ref[e].astype(F32) + bu_in[e].astype(F32) + bd_in[e].astype(F32))

            @pl.when(q_in & (l < n - 1))
            def _():
                b_up(q).start()

            @pl.when(p_in_ & (l > 0))
            def _():
                b_dn(p).start()


        def x_send(c, i, v):
            where = pl.ds(i * g, g)
            return remote(x_out.at[c, v, where], x_in.at[c, w, where], xs.at[(c * groups + i) * w_count + v],
                          xr.at[(c * groups + i) * w_count + w], wid=v)

        def x_landed(c, i, v):
            where = pl.ds(i * g, g)
            return remote(x_in.at[c, v, where], x_in.at[c, v, where],
                          xs.at[(c * groups + i) * w_count + v],
                          xr.at[(c * groups + i) * w_count + v], wid=v)

        def slot_group(c, i):
            for k in [i * g + d for d in range(g)]:
                held = e_ref[tab[at.tgt + k], :, chunk(c), :].reshape(rows, width)
                back = lax.dot_general(
                    held, w_ref[k], (((1,), (1,)), ((), ())), preferred_element_type=F32
                ).astype(BF16).reshape(w_count, ct, block)
                for v in range(w_count):
                    x_out[c, v, k] = back[v]
            others(w, w_count, lambda v: x_send(c, i, v).start())

        def gather(c):
            def landed(i, carry):
                others(w, w_count, lambda v: x_landed(c, i, v).wait_recv())
                return carry

            lax.fori_loop(0, groups, landed, 0)

            def one(k, carry):
                total = c_sums[tab[at.prev_id + k]] + x_out[c, w, k].astype(F32)
                for d in range(1, w_count):
                    total = total + x_in[c, lax.rem(w + d, w_count), k].astype(F32)
                c_sums[k + 1] = total
                return carry

            lax.fori_loop(0, slots, one, 0)

            def out(b, carry):
                made[c, b] = c_sums[tab[at.last_id + b]].astype(BF16)
                return carry

            lax.fori_loop(0, blocks, out, 0)

        def z_up(q):
            return remote(zu_out.at[q], zu_in.at[q], zus.at[q], zur.at[q], lay=l + 1)

        def z_dn(q):
            return remote(zd_out.at[q], zd_in.at[q], zds.at[q], zdr.at[q], lay=l - 1)

        def z_inside(q):
            return (q >= 0) & (q < chunks * period) & (lax.rem(q + period * chunks, period) < z_steps)

        def z_piece(q):
            return q // period * z_steps + lax.rem(q + period * chunks, period)

        def own_z(q, dest):
            return made[q // z_steps, pl.ds(dest * per_dev + lax.rem(q, split) * pb, pb)].astype(F32)

        def twin_pre(c):
            return remote(twin_out.at[c], po_ref.at[r, chunk(c)], tps.at[c], tpr.at[c], rep=twin)

        def twin_landed(c):
            return remote(twin_out.at[c], po_ref.at[twin, chunk(c)], tps.at[c], tpr.at[c], rep=twin)

        def reduce_on(s):
            q, p = s - Z_SKEW * l, s - Z_SKEW * (n - 1 - l)
            q_in, p_in_ = z_inside(q), z_inside(p)
            q, p = z_piece(q), z_piece(p)
            to_up = n - 1 - lax.rem(q + z_pieces, z_steps) // split
            to_dn = lax.rem(p + z_pieces, z_steps) // split

            @pl.when(q_in & (l > 0) & (to_up >= l))
            def _():
                remote(zu_in.at[q], zu_in.at[q], zus.at[q], zur.at[q], lay=l).wait_recv()

            @pl.when(q_in & (l == 0))
            def _():
                zu_out[q] = own_z(q, to_up).astype(BF16)

            @pl.when(q_in & (l > 0) & (to_up > l))
            def _():
                zu_out[q] = (own_z(q, to_up) + zu_in[q].astype(F32)).astype(BF16)

            @pl.when(p_in_ & (l < n - 1) & (to_dn <= l))
            def _():
                remote(zd_in.at[p], zd_in.at[p], zds.at[p], zdr.at[p], lay=l).wait_recv()

            @pl.when(p_in_ & (l == n - 1))
            def _():
                zd_out[p] = own_z(p, to_dn).astype(BF16)

            @pl.when(p_in_ & (l < n - 1) & (to_dn < l))
            def _():
                zd_out[p] = (own_z(p, to_dn) + zd_in[p].astype(F32)).astype(BF16)

            off_up = (n - 1 - l) * split
            off_dn = l * split
            f = s - jnp.maximum(off_up + Z_SKEW * l, off_dn + Z_SKEW * (n - 1 - l))
            i = lax.rem(f + period * chunks, period)
            whole = (f >= 0) & (f < chunks * period) & (i < split)
            c = f // period

            def finish(total):
                blocks_here = pl.ds(i * pb, pb)
                grad = (total * sl_ref[blocks_here, chunk(c), :]).astype(BF16)
                if split == r_count:
                    @pl.when(i == r)
                    def _():
                        for b in range(pb):
                            po_ref[r, chunk(c), b * block:(b + 1) * block] = grad[b]

                    @pl.when(i != r)
                    def _():
                        for b in range(pb):
                            twin_out[c, :, b * block:(b + 1) * block] = grad[b]
                else:
                    for b in range(pb):
                        for side in range(r_count):
                            cut = grad[b][:, side * half:(side + 1) * half]

                            @pl.when(r == side)
                            def _():
                                po_ref[side, chunk(c), b * half:(b + 1) * half] = cut

                            @pl.when(r != side)
                            def _():
                                twin_out[c, :, b * half:(b + 1) * half] = cut

            def mid():
                return made[c, pl.ds(l * per_dev + i * pb, pb)].astype(F32)

            @pl.when(whole & (l == 0))
            def _():
                finish(mid() + zd_in[c * z_steps + off_dn + i].astype(F32))

            @pl.when(whole & (l == n - 1))
            def _():
                finish(mid() + zu_in[c * z_steps + off_up + i].astype(F32))

            @pl.when(whole & (l > 0) & (l < n - 1))
            def _():
                finish(mid() + zu_in[c * z_steps + off_up + i].astype(F32)
                       + zd_in[c * z_steps + off_dn + i].astype(F32))

            @pl.when(q_in & (to_up > l))
            def _():
                z_up(q).start()

            @pl.when(p_in_ & (to_dn < l))
            def _():
                z_dn(p).start()

            @pl.when(whole & (i == split - 1))
            def _():
                twin_pre(c).start()


        twins = [
            remote(lat_ref.at[:, :, :, pl.ds(pl.multiple_of(twin * half, half), half)], lo_ref,
                   ts.at[0], tr.at[0], rep=twin),
            remote(e_ref, eo_ref, ts.at[1], tr.at[1], rep=twin),
        ] + [
            remote(a_ref.at[v], ao_ref.at[lax.rem(v - w + w_count, w_count), r], ts.at[2 + v], tr.at[2 + v],
                   rep=twin)
            for v in range(w_count)
        ]
        mine = [
            pltpu.make_async_copy(lat_ref, lat_hbm, asem.at[0]),
            pltpu.make_async_copy(e_ref, e_hbm, asem.at[1]),
        ] + [
            pltpu.make_async_copy(
                a_ref.at[v], ao_ref.at[lax.rem(v - w + w_count, w_count), r], asem.at[2 + v])
            for v in range(w_count)
        ]

        def tick(s, carry):
            def arrive(d):
                at_chunk(s, A_GATE + A_SKEW * d, lambda c: nearest(l, n, d, lambda j: take(c, j)))

            loop(1, n, arrive)
            hand_on(s - b_first)
            at_chunk(s, c_gather, gather)
            reduce_on(s - c_gather)
            at_chunk(s, A_GATE, gated)
            at_chunk(s, 0, product)

            t = s - c_slots

            @pl.when((t >= 0) & (t < chunks * period))
            def _():
                c, i = t // period, lax.rem(t, period)
                lax.fori_loop(
                    (i * groups + period - 1) // period, ((i + 1) * groups + period - 1) // period,
                    lambda j, z: (slot_group(c, j), z)[1], 0,
                )

            u = s - a_decode

            @pl.when((u >= 0) & (u < chunks * period))
            def _():
                c, i = u // period, lax.rem(u, period)

                @pl.when(i == 0)
                def _():
                    crossed(c)

                for d in range(per_step):
                    @pl.when(i * per_step + d < slots)
                    def _():
                        slot(i * per_step + d)

                @pl.when(i == period - 1)
                def _():
                    emit(c)

            @pl.when(s == a_decode - 1)
            def _():
                loop(0, slots, lambda k: weight(k).wait())
                for v in range(w_count):
                    twins[2 + v].start()
                    mine[2 + v].start()

            @pl.when(s == a_decode + (chunks - 1) * period)
            def _():
                twins[0].start()
                mine[0].start()

            @pl.when(s == c_slots + (chunks - 1) * period)
            def _():
                twins[1].start()
                mine[1].start()

            return carry

        lax.fori_loop(0, ticks, tick, 0)

        def a_sent(q, carry):
            goes(q // n, lax.rem(q, n), lambda copy: copy.wait_send())
            return carry

        lax.fori_loop(0, chunks * n, a_sent, 0)

        def b_sent(q, carry):
            @pl.when(l < n - 1)
            def _():
                b_up(q).wait_send()

            @pl.when(l > 0)
            def _():
                b_dn(q).wait_send()

            return carry

        lax.fori_loop(0, b_pieces, b_sent, 0)

        def z_sent(q, carry):
            to_up = n - 1 - lax.rem(q, z_steps) // split
            to_dn = lax.rem(q, z_steps) // split

            @pl.when(to_up > l)
            def _():
                z_up(q).wait_send()

            @pl.when(to_dn < l)
            def _():
                z_dn(q).wait_send()

            return carry

        lax.fori_loop(0, z_pieces, z_sent, 0)

        def x_sent(q, carry):
            others(w, w_count, lambda v: x_send(q // groups, lax.rem(q, groups), v).wait_send())
            return carry

        lax.fori_loop(0, chunks * groups, x_sent, 0)
        for c in range(chunks):
            others(w, w_count, lambda v: p_send(c, v).wait_send())
            twin_landed(c).wait()
        for copy in twins + mine:
            copy.wait()

    b_piece_shape = (b_pieces, rows, part)
    z_piece_shape = (z_pieces, pb, ct, block)
    x_shape = (chunks, w_count, slots, ct, block)
    lat_shape = (blocks, w_count, toks, block)
    vmem = pl.BlockSpec(memory_space=pltpu.VMEM)
    dma = pltpu.SemaphoreType.DMA
    x_sems = chunks * groups * w_count
    return pl.pallas_call(
        body,
        out_shape=(
            jax.ShapeDtypeStruct((r_count, toks, columns), BF16),
            jax.ShapeDtypeStruct(lat_shape, BF16),
            jax.ShapeDtypeStruct(lat_shape[:3] + (half,), BF16),
            jax.ShapeDtypeStruct(targets.shape, BF16),
            jax.ShapeDtypeStruct(targets.shape, BF16),
            jax.ShapeDtypeStruct((w_count, r_count, toks, width), acts_here.dtype),
        ),
        in_specs=[pl.BlockSpec(memory_space=pltpu.SMEM), vmem, vmem, vmem, vmem, ANY, vmem],
        out_specs=(vmem, ANY, ANY, ANY, ANY, ANY),
        scratch_shapes=[
            pltpu.VMEM(dec_weight.shape, BF16),
            pltpu.VMEM(lat_shape, BF16),
            pltpu.VMEM((blocks, w_count, ct, block), BF16),
            pltpu.VMEM((per_dev, toks, block), F32),
            pltpu.VMEM((chunks, w_count, ct, lat_dev), BF16),
            pltpu.VMEM((chunks, w_count, ct, lat_dev), BF16),
            pltpu.VMEM(targets.shape, BF16),
            pltpu.VMEM((slots + 1, rows, width), F32),
        ] + [pltpu.VMEM(b_piece_shape, BF16)] * 5 + [
            pltpu.VMEM(x_shape, BF16),
            pltpu.VMEM(x_shape, BF16),
            pltpu.VMEM((slots + 1, ct, block), F32),
            pltpu.VMEM((chunks, blocks, ct, block), BF16),
        ] + [pltpu.VMEM(z_piece_shape, BF16)] * 4 + [
            pltpu.VMEM((chunks, ct, columns), BF16),
            dma((slots,)), dma((chunks * w_count,)), dma((chunks * w_count,)),
        ] + [dma((chunks * n,))] * 3 + [dma((chunks * n * w_count,))] * 2 + [dma((b_pieces,))] * 4
        + [dma((x_sems,))] * 2 + [dma((z_pieces,))] * 4 + [
            dma((2 + w_count,)), dma((2 + w_count,)), dma((chunks,)), dma((chunks,)), dma((2 + w_count,)),
        ],
        compiler_params=pltpu.CompilerParams(
            collective_id=cid, has_side_effects=True, vmem_limit_bytes=67043328
        ),
        name="step",
    )(tables, acts_here, enc_weight, enc_bias, gate, dec_weight, targets)


def decoder_grads(ids, tgt, valid, rep, lat, lat_twin, err, err_twin, slots):
    layers, toks, width = err.shape
    blocks, _, half = lat_twin.shape
    g = group_of(slots)

    def body(i_ref, t_ref, v_ref, r_ref, l_ref, lt_ref, e_ref, et_ref, o_ref):
        over = (((0,), (0,)), ((), ()))
        for i in range(g):
            k = pl.program_id(0) * g + i

            @pl.when(v_ref[k] > 0)
            def _():
                t, b = t_ref[k], i_ref[k]
                o_ref[i] = lax.dot_general(
                    l_ref[b], e_ref[t], over, preferred_element_type=F32
                ) + lax.dot_general(lt_ref[b], et_ref[t], over, preferred_element_type=F32)

            @pl.when(v_ref[k] == 0)
            def _():
                o_ref[i] = jnp.zeros_like(o_ref[i])

    return slot_call(
        body, (ids, tgt, valid, rep), (lat, lat_twin, err, err_twin),
        [pl.BlockSpec((blocks, toks, half), lambda k, i, t, v, r: (0, 0, r[0])),
         pl.BlockSpec((blocks, toks, half), lambda k, i, t, v, r: (0, 0, 0)),
         pl.BlockSpec((layers, toks, width), lambda k, i, t, v, r: (0, 0, 0)),
         pl.BlockSpec((layers, toks, width), lambda k, i, t, v, r: (0, 0, 0))],
        jax.ShapeDtypeStruct((slots, half, width), F32),
        pl.BlockSpec((g, half, width), lambda k, i, t, v, r: (k, 0, 0)),
        [], 4 * slots * toks * half * width, "decoder_grads", slots // g,
    )


def local(acts, targets, enc_weight, enc_bias, gate_mask, dec_list, dec_weight):
    layers, tok_rows, width_part = acts.shape
    lat_dev = enc_weight.shape[1]
    slots, block, _ = dec_weight.shape
    per_dev = lat_dev // block
    n, w_count, r_count = lax.axis_size("lay"), lax.axis_size("wid"), lax.axis_size("rep")
    lay, wid, rep = lax.axis_index("lay"), lax.axis_index("wid"), lax.axis_index("rep")
    lat_total = lat_dev * n
    blocks_total = lat_total // block
    latents_layer = lat_total // layers
    blocks_layer = latents_layer // block
    toks = tok_rows // w_count

    tgt = dec_list[:, 1]
    valid = (tgt >= 0).astype(jnp.int32)
    ids = jnp.maximum(dec_list[:, 0] * blocks_layer + dec_list[:, 2], 0)
    tgt = jnp.maximum(tgt, 0)

    here = lax.dynamic_index_in_dim(acts, lay * lat_dev // latents_layer, 0, keepdims=False)
    here = here.reshape(w_count, toks, width_part)
    scale = float(tok_rows * r_count) ** (-0.5)
    pre_mine, lat, lat_twin, err, err_twin, acts_all = step(
        slot_tables(dec_list, layers, blocks_total, blocks_layer), here, enc_weight,
        enc_bias.reshape(1, lat_dev), gate_mask.reshape(w_count, toks, per_dev), dec_weight,
        targets.reshape(layers, w_count, toks, width_part), scale, 0,
    )
    pre_all = [pre_mine] + [
        lax.ppermute(pre_mine, "wid", [(i, (i - d) % w_count) for i in range(w_count)])
        for d in range(1, w_count)
    ]
    half = block // r_count
    dec_out = decoder_grads(
        ids, tgt, valid, rep.reshape(1).astype(jnp.int32),
        lat.reshape(blocks_total, tok_rows, block), lat_twin.reshape(blocks_total, tok_rows, half),
        err.reshape(layers, tok_rows, width_part), err_twin.reshape(layers, tok_rows, width_part), slots,
    )
    columns = lat_dev // r_count
    pre_all = jnp.stack(pre_all).reshape(r_count * tok_rows, columns)
    enc_out = lax.dot_general(
        acts_all.reshape(r_count * tok_rows, width_part), pre_all, (((0,), (0,)), ((), ())),
        preferred_element_type=F32,
    )
    bias_out = jnp.sum(pre_all.astype(F32), axis=0)
    return (enc_out, bias_out, dec_out)


def solution(mesh):
    return jax.shard_map(
        local,
        mesh=mesh,
        in_specs=(
            P(None, ("grp", "rep"), "wid"),
            P(None, ("grp", "rep"), "wid"),
            P("wid", "lay"),
            P("lay"),
            P(("grp", "rep"), "lay"),
            P("lay", None),
            P("lay", None, "wid"),
        ),
        out_specs=(
            P(("grp", "wid"), ("lay", "rep")),
            P(("grp", "lay", "rep")),
            P(("grp", "lay"), "rep", "wid"),
        ),
        check_vma=False,
    )
```

time: 226 us -> 184 us (0.81)
  Pallas kernels: 205 us -> 169 us
  matrix products: 9.13 us -> 4.53 us
    pallas_call x4 -> x1, Pallas kernels: 189 us -> 152 us  [step(): pl.pallas_call(body, out_shape=(jax.ShapeDtypeStruct((r_count, toks, colu...]
    dot_general x1 -> x0, matrix products: 4.6 us -> none  [local(): partial = jnp.dot(here, enc_weight, preferred_element_type=F32).astype(BF16)]
  transfers between devices with their start and end apart: 1 -> 1, of which waited for: 0 -> 0; matrix products, arithmetic and copies ran while one was open for 0% -> 1% of each run, Pallas kernels for 6% -> 7%
where the time goes in v3:
time: 184 us
  Pallas kernels  169 us (92%)
  local copies, waits for them, and re-layouts  4.73 us (3%)
  matrix products  4.53 us (2%)
  other arithmetic  3.36 us (2%)
    pallas_call x1, Pallas kernels, step(): pl.pallas_call(body, out_shape=(jax.ShapeDtypeStruct((r_count, toks, colu...  152 us
    pallas_call x1, Pallas kernels, slot_call(): pl.pallas_call(body, out_shape=out_shape, grid_spec=pltpu.PrefetchScalarG...  12.9 us
    dot_general x1, matrix products, local(): lax.dot_general(acts_all.reshape(r_count * tok_rows, width_part), pre_all...  4.53 us
  transfers between devices with their start and end apart: 1, of which 0 were waited for; matrix products, arithmetic and copies ran while one was open for 1% of the time, Pallas kernels for 7%

profile of v3, /device:TPU:0, one launch (start us, length us, event | category | flops | bytes accessed | tf_op | source)
XLA Modules:
  0.0 183.8 jit_solution(11752762939838665893)
XLA Ops:
  0.6 1.4 copy.10.d_ref
  2.0 3.4 %slot_tables.1.tab = s32[256]{0:T(256)} custom-call(s32[21,3]{1,0:T(8,128)} %copy.10.d_ref), custom_call_target="tpu_custom_call" | custom-call | tf_op jit(solution)/shard_map/slot_tables/pallas_call | solution.py:124
  5.4 1.5 copy.11
  6.9 1.9 %constant_dynamic-slice_fusion = bf16[1,256,1024]{2,1,0:T(8,128)(2,1)} fusion(bf16[4,256,1024]{2,1,0:T(8,128)(2,1)} %param.7, s32[]{:T(128)S(6)} %select_n.10), kind=kLoop, calls=%fused_computation.7 | loop fusion | bytes 1048580 | tf_op jit(solution)/shard_map/jit(dynamic_index_in_dim)/dynamic_slice | solution.py:728
  8.8 152.4 %step.1 = (bf16[2,128,1024]{2,1,0:T(8,128)(2,1)}, bf16[32,2,128,256]{3,2,1,0:T(8,128)(2,1)}, bf16[32,2,128,128]{3,2,1,0:T(8,128)(2,1)}, bf16[4,2,128,1024]{3,2,1...) custom-call(s32[256]{0:T(256)} %slot_tables.1.tab, ...), custom_call_target="tpu_custom_call" | custom-call | tf_op jit(solution)/shard_map/step/pallas_call | solution.py:637
  161.2 1.8 collective-permute-start
  163.0 1.3 fusion.v_ref
  164.3 1.3 maximum_bitcast_fusion
  165.6 0.0 copy-start
  165.6 12.9 %decoder_grads.1 = f32[21,128,1024]{2,1,0:T(8,128)} custom-call(s32[21]{0:T(128)} %get-tuple-element.16.i_ref, s32[21]{0:T(128)} %get-tuple-element.15.t_ref, s32[21]{0:T(128)} %fusion.v_ref, s32[1]{0:T(128)} %bitcast.11.r_ref, bf16[32,256,256]{2,1,0:T(8,128)(2,1)} %bitcast.22, bf16[32,256,128]{2,1,0:T(8,128)(2,1)} %bitcast.29, ...), custom_call_target="tpu_custom_call" | custom-call | flops 2818572288 | bytes 21495808 | tf_op jit(solution)/shard_map/decoder_grads/pallas_call | solution.py:75
  178.5 0.0 collective-permute-done
  178.5 0.0 copy-done
  178.5 0.8 convert_reduce_fusion
  179.3 4.5 %convolution_bitcast_fusion = f32[1024,1024]{1,0:T(8,128)} fusion(bf16[2,2,128,1024]{3,2,1,0:T(8,128)(2,1)} %get-tuple-element.9, bf16[1,2,128,1024]{3,2,1,0:T(8,128)(2,1)S(1)} %bitcast.26, bf16[1,2,128,1024]{3,2,1,0:T(8,128)(2,1)S(1)} %bitcast.24), kind=kOutput, calls=%fused_computation | convolution fusion | flops 1074266112 | bytes 6291456 | tf_op jit(solution)/shard_map/dot_general | solution.py:748
Async XLA Ops:
  161.2 17.3 %collective-permute-start = (bf16[2,128,1024]{2,1,0:T(8,128)(2,1)}, bf16[2,128,1024]{2,1,0:T(8,128)(2,1)S(1)}, u32[]{:S(2)}, u32[]{:S(2)}) collective-permute-start(bf16[2,128,1024]{2,1,0:T(8,128)(2,1)} %get-tuple-element.10), channel_id=1, source_target_pairs={{0,2},{2,0},{1,3},{3,1},{4,6},{6,4},{5,7},{7,5},{8,10},{10,8},{9,1... | collective-permute-start | bytes 1572872 | tf_op jit(solution)/shard_map/ppermute | solution.py:737
  165.6 12.9 %copy-start = (bf16[2,128,1024]{2,1,0:T(8,128)(2,1)S(1)}, bf16[2,128,1024]{2,1,0:T(8,128)(2,1)}, u32[]{:S(2)}) copy-start(bf16[2,128,1024]{2,1,0:T(8,128)(2,1)} %get-tuple-element.10) | copy-start | bytes 1572868

commit v4 on v3

--- a/solution.py
+++ b/solution.py
@@ -11,11 +11,12 @@
 BF16 = jnp.bfloat16
 F32 = jnp.float32
 CUTS = 2
-SKEW = 3
-Z_SKEW = 3
-A_GATE = 3
+SKEW = 4
+Z_SKEW = 5
+PERIOD = 8
+A_GATE = 14
 A_SKEW = 3
-A_ACROSS = 3
+A_ACROSS = 7
 C_ACROSS = 3
 
 
@@ -87,62 +88,26 @@
 
 class Tables:
     def __init__(self, slots, layers, blocks):
-        self.tgt, self.id, self.valid = 0, slots, 2 * slots
+        self.tgt, self.id, self.raw = 0, slots, 2 * slots
         self.prev_tgt, self.prev_id = 3 * slots, 4 * slots
         self.last_tgt = 5 * slots
-        self.last_id = self.last_tgt + layers + 1
-        self.size = -(-(self.last_id + blocks + 1) // 128) * 128
-
-
-def slot_tables(dec_list, layers, blocks, blocks_layer):
-    slots = dec_list.shape[0]
-    at = Tables(slots, layers, blocks)
-
-    def body(d_ref, o_ref):
-        def clear(i, c):
-            o_ref[i] = 0
-            return c
-
-        lax.fori_loop(0, at.size, clear, 0)
-
-        def one(k, c):
-            s, t, b = d_ref[k, 0], d_ref[k, 1], d_ref[k, 2]
-            listed = t >= 0
-            group = jnp.where(listed, t, layers)
-            ident = jnp.where(listed, s * blocks_layer + b, blocks)
-            o_ref[at.tgt + k] = jnp.maximum(t, 0)
-            o_ref[at.id + k] = jnp.where(listed, ident, 0)
-            o_ref[at.valid + k] = jnp.where(listed, 1, 0)
-            o_ref[at.prev_tgt + k] = o_ref[at.last_tgt + group]
-            o_ref[at.last_tgt + group] = k + 1
-            o_ref[at.prev_id + k] = o_ref[at.last_id + ident]
-            o_ref[at.last_id + ident] = k + 1
-            return c
-
-        lax.fori_loop(0, slots, one, 0)
-
-    return pl.pallas_call(
-        body,
-        out_shape=jax.ShapeDtypeStruct((at.size,), jnp.int32),
-        in_specs=[pl.BlockSpec(memory_space=pltpu.SMEM)],
-        out_specs=pl.BlockSpec(memory_space=pltpu.SMEM),
-        name="slot_tables",
-    )(dec_list)
+        self.last_id = self.last_tgt + layers
+        self.size = -(-(self.last_id + blocks) // 128) * 128
 
 
 def chunk_count(toks):
     return next(c for c in (4, 2, 1) if toks % (16 * c) == 0 or c == 1)
 
 
-def step(tables, acts_here, enc_weight, enc_bias, gate, dec_weight, targets, scale, cid):
-    w_count, toks, width = acts_here.shape
+def step(acts, enc_weight, enc_bias, gate, dec_list, dec_weight, targets, scale, cid):
+    layers, w_count, toks, width = acts.shape
     lat_dev = enc_weight.shape[1]
     slots, block, _ = dec_weight.shape
-    layers = targets.shape[0]
     per_dev = lat_dev // block
     n, r_count = lax.axis_size("lay"), lax.axis_size("rep")
     assert r_count == 2
     blocks = n * per_dev
+    blocks_layer = blocks // layers
     columns = lat_dev // r_count
     half = block // r_count
     at = Tables(slots, layers, blocks)
@@ -163,7 +128,7 @@
     g = group_of(slots)
     groups = slots // g
 
-    period = max(b_steps, z_steps)
+    period = max(b_steps, z_steps, PERIOD)
     per_step = -(-slots // period)
     a_decode = A_GATE + A_SKEW * (n - 1) + A_ACROSS
     b_first = a_decode + period
@@ -171,18 +136,30 @@
     c_gather = c_slots + period + C_ACROSS
     ticks = c_gather + (chunks - 1) * period + split + (n - 1) * max(split, Z_SKEW)
 
-    def body(tab, a_ref, ew_ref, b_ref, g_ref, w_hbm, t_ref,
-             po_ref, lat_hbm, lo_ref, e_hbm, eo_ref, ao_ref,
-             w_ref, lat_ref, lat_now, sl_ref, p_out, p_in, e_ref, sums, own_ref, bu_in, bd_in, bu_out, bd_out,
+    table_slots = -(-slots // (a_decode - 1))
+    table_blocks = -(-blocks // (a_decode - 1))
+
+    def body(d_ref, a_hbm, ew_hbm, b_ref, g_ref, w_hbm, t_ref,
+             tab, po_ref, lo_ref, eo_ref, ao_ref,
+             a_ref, ew_ref, keep_ref, w_ref, lat_ref, lat_now, sl_ref, p_out, p_in, e_ref, sums, own_ref, bu_in, bd_in, bu_out, bd_out,
              x_out, x_in, c_sums, made, zu_in, zd_in, zu_out, zd_out, twin_out,
              wsem, ps, pr, aus, ads, azr, axs, axr, bus, bur, bds, bdr, xs, xr, zus, zur, zds, zdr,
-             ts, tr, tps, tpr, asem):
+             ts, tr, tps, tpr, asem, isem):
         l, w, r = lax.axis_index("lay"), lax.axis_index("wid"), lax.axis_index("rep")
         twin = 1 - r
 
         def weight(k):
             return pltpu.make_async_copy(w_hbm.at[k], w_ref.at[k], wsem.at[k])
 
+        layer = l * per_dev // blocks_layer
+        acts_in = pltpu.make_async_copy(a_hbm.at[layer], a_ref, isem.at[0])
+        enc_in = [
+            pltpu.make_async_copy(ew_hbm.at[:, o:o + wide], ew_ref.at[:, o:o + wide], isem.at[1 + i])
+            for i, o in enumerate(range(0, lat_dev, wide))
+        ]
+        acts_in.start()
+        for copy in enc_in:
+            copy.start()
         loop(0, slots, lambda k: weight(k).start())
         barrier = pltpu.get_barrier_semaphore()
         others(l, n, lambda j: signal(barrier, lay=j))
@@ -190,7 +167,51 @@
         signal(barrier, rep=twin)
         sums[0] = jnp.zeros_like(sums[0])
         c_sums[0] = jnp.zeros_like(c_sums[0])
+        keep_ref[...] = g_ref[...].astype(F32).T
+
+        def listed(k, carry):
+            t = d_ref[1, k]
+            raw = jnp.where(t >= 0, d_ref[0, k] * blocks_layer + d_ref[2, k], -1)
+            tab[at.tgt + k] = jnp.maximum(t, 0)
+            tab[at.raw + k] = raw
+            tab[at.id + k] = jnp.maximum(raw, 0)
+            return carry
+
+        lax.fori_loop(0, slots, listed, 0)
+
+        def last_of(which, value, below):
+            found = jnp.int32(0)
+            for j in range(slots):
+                found = jnp.where((which(j) == value) & (j < below), j + 1, found)
+            return found
+
+        def target(j):
+            return d_ref[1, j]
+
+        def named(j):
+            return tab[at.raw + j]
+
+        for t in range(layers):
+            tab[at.last_tgt + t] = last_of(target, t, slots)
+
+        def some_tables(s):
+            for d in range(table_slots):
+                k = s * table_slots + d
+
+                @pl.when(k < slots)
+                def _():
+                    tab[at.prev_tgt + k] = last_of(target, target(k), k)
+                    tab[at.prev_id + k] = last_of(named, named(k), k)
+
+            for d in range(table_blocks):
+                b = s * table_blocks + d
+
+                @pl.when(b < blocks)
+                def _():
+                    tab[at.last_id + b] = last_of(named, b, slots)
+
         pl.semaphore_wait(barrier, n + w_count - 1)
+        acts_in.wait()
 
         def chunk(c):
             return pl.ds(pl.multiple_of(c * ct, ct), ct)
@@ -213,7 +234,11 @@
 
         def product(c):
             held = a_ref[:, chunk(c), :].reshape(rows, width)
-            for o in range(0, lat_dev, wide):
+            for i, o in enumerate(range(0, lat_dev, wide)):
+                @pl.when(c == 0)
+                def _():
+                    enc_in[i].wait()
+
                 made_here = jnp.dot(held, ew_ref[:, o:o + wide], preferred_element_type=F32).astype(BF16)
                 for v in range(w_count):
                     p_out[c, v, :, o:o + wide] = made_here[v * ct:(v + 1) * ct]
@@ -245,7 +270,7 @@
 
         def gated(c):
             others(w, w_count, lambda v: p_landed(c, v).wait_recv())
-            keep = g_ref[w, chunk(c), :].astype(F32)
+            keep = keep_ref[pl.ds(pl.multiple_of(w * toks + c * ct, ct), ct), :]
             for b in range(per_dev):
                 over = slice(b * block, (b + 1) * block)
                 shifted = p_out[c, w, :, over].astype(F32) + b_ref[:, over]
@@ -503,17 +528,18 @@
 
 
         twins = [
-            remote(lat_ref.at[:, :, :, pl.ds(pl.multiple_of(twin * half, half), half)], lo_ref,
+            remote(lat_ref.at[:, :, :, pl.ds(pl.multiple_of(twin * half, half), half)], lo_ref.at[:, r],
                    ts.at[0], tr.at[0], rep=twin),
-            remote(e_ref, eo_ref, ts.at[1], tr.at[1], rep=twin),
+            remote(e_ref, eo_ref.at[:, r], ts.at[1], tr.at[1], rep=twin),
         ] + [
             remote(a_ref.at[v], ao_ref.at[lax.rem(v - w + w_count, w_count), r], ts.at[2 + v], tr.at[2 + v],
                    rep=twin)
             for v in range(w_count)
         ]
         mine = [
-            pltpu.make_async_copy(lat_ref, lat_hbm, asem.at[0]),
-            pltpu.make_async_copy(e_ref, e_hbm, asem.at[1]),
+            pltpu.make_async_copy(
+                lat_ref.at[:, :, :, pl.ds(pl.multiple_of(r * half, half), half)], lo_ref.at[:, r], asem.at[0]),
+            pltpu.make_async_copy(e_ref, eo_ref.at[:, r], asem.at[1]),
         ] + [
             pltpu.make_async_copy(
                 a_ref.at[v], ao_ref.at[lax.rem(v - w + w_count, w_count), r], asem.at[2 + v])
@@ -531,6 +557,10 @@
             at_chunk(s, A_GATE, gated)
             at_chunk(s, 0, product)
 
+            @pl.when(s < a_decode - 1)
+            def _():
+                some_tables(s)
+
             t = s - c_slots
 
             @pl.when((t >= 0) & (t < chunks * period))
@@ -632,21 +662,24 @@
     x_shape = (chunks, w_count, slots, ct, block)
     lat_shape = (blocks, w_count, toks, block)
     vmem = pl.BlockSpec(memory_space=pltpu.VMEM)
+    smem = pl.BlockSpec(memory_space=pltpu.SMEM)
     dma = pltpu.SemaphoreType.DMA
     x_sems = chunks * groups * w_count
     return pl.pallas_call(
         body,
         out_shape=(
+            jax.ShapeDtypeStruct((at.size,), jnp.int32),
             jax.ShapeDtypeStruct((r_count, toks, columns), BF16),
-            jax.ShapeDtypeStruct(lat_shape, BF16),
-            jax.ShapeDtypeStruct(lat_shape[:3] + (half,), BF16),
-            jax.ShapeDtypeStruct(targets.shape, BF16),
-            jax.ShapeDtypeStruct(targets.shape, BF16),
-            jax.ShapeDtypeStruct((w_count, r_count, toks, width), acts_here.dtype),
+            jax.ShapeDtypeStruct((blocks, r_count, w_count, toks, half), BF16),
+            jax.ShapeDtypeStruct((layers, r_count, w_count, toks, width), BF16),
+            jax.ShapeDtypeStruct((w_count, r_count, toks, width), BF16),
         ),
-        in_specs=[pl.BlockSpec(memory_space=pltpu.SMEM), vmem, vmem, vmem, vmem, ANY, vmem],
-        out_specs=(vmem, ANY, ANY, ANY, ANY, ANY),
+        in_specs=[smem, ANY, ANY, vmem, vmem, ANY, vmem],
+        out_specs=(smem, vmem, ANY, ANY, ANY),
         scratch_shapes=[
+            pltpu.VMEM((w_count, toks, width), BF16),
+            pltpu.VMEM(enc_weight.shape, BF16),
+            pltpu.VMEM((w_count * toks, per_dev), F32),
             pltpu.VMEM(dec_weight.shape, BF16),
             pltpu.VMEM(lat_shape, BF16),
             pltpu.VMEM((blocks, w_count, ct, block), BF16),
@@ -666,88 +699,69 @@
         ] + [dma((chunks * n,))] * 3 + [dma((chunks * n * w_count,))] * 2 + [dma((b_pieces,))] * 4
         + [dma((x_sems,))] * 2 + [dma((z_pieces,))] * 4 + [
             dma((2 + w_count,)), dma((2 + w_count,)), dma((chunks,)), dma((chunks,)), dma((2 + w_count,)),
+            dma((1 + lat_dev // wide,)),
         ],
         compiler_params=pltpu.CompilerParams(
             collective_id=cid, has_side_effects=True, vmem_limit_bytes=67043328
         ),
         name="step",
-    )(tables, acts_here, enc_weight, enc_bias, gate, dec_weight, targets)
-
-
-def decoder_grads(ids, tgt, valid, rep, lat, lat_twin, err, err_twin, slots):
+    )(dec_list, acts, enc_weight, enc_bias, gate, dec_weight, targets)
+
+
+def decoder_grads(tables, lat, err, slots):
     layers, toks, width = err.shape
-    blocks, _, half = lat_twin.shape
+    blocks, _, half = lat.shape
     g = group_of(slots)
-
-    def body(i_ref, t_ref, v_ref, r_ref, l_ref, lt_ref, e_ref, et_ref, o_ref):
-        over = (((0,), (0,)), ((), ()))
+    at = Tables(slots, layers, blocks)
+
+    def body(tab, l_ref, e_ref, o_ref):
         for i in range(g):
             k = pl.program_id(0) * g + i
 
-            @pl.when(v_ref[k] > 0)
-            def _():
-                t, b = t_ref[k], i_ref[k]
+            @pl.when(tab[at.raw + k] >= 0)
+            def _():
                 o_ref[i] = lax.dot_general(
-                    l_ref[b], e_ref[t], over, preferred_element_type=F32
-                ) + lax.dot_general(lt_ref[b], et_ref[t], over, preferred_element_type=F32)
-
-            @pl.when(v_ref[k] == 0)
+                    l_ref[tab[at.id + k]], e_ref[tab[at.tgt + k]], (((0,), (0,)), ((), ())),
+                    preferred_element_type=F32,
+                )
+
+            @pl.when(tab[at.raw + k] < 0)
             def _():
                 o_ref[i] = jnp.zeros_like(o_ref[i])
 
     return slot_call(
-        body, (ids, tgt, valid, rep), (lat, lat_twin, err, err_twin),
-        [pl.BlockSpec((blocks, toks, half), lambda k, i, t, v, r: (0, 0, r[0])),
-         pl.BlockSpec((blocks, toks, half), lambda k, i, t, v, r: (0, 0, 0)),
-         pl.BlockSpec((layers, toks, width), lambda k, i, t, v, r: (0, 0, 0)),
-         pl.BlockSpec((layers, toks, width), lambda k, i, t, v, r: (0, 0, 0))],
+        body, (tables,), (lat, err),
+        [pl.BlockSpec((blocks, toks, half), lambda k, t: (0, 0, 0)),
+         pl.BlockSpec((layers, toks, width), lambda k, t: (0, 0, 0))],
         jax.ShapeDtypeStruct((slots, half, width), F32),
-        pl.BlockSpec((g, half, width), lambda k, i, t, v, r: (k, 0, 0)),
-        [], 4 * slots * toks * half * width, "decoder_grads", slots // g,
+        pl.BlockSpec((g, half, width), lambda k, t: (k, 0, 0)),
+        [], 2 * slots * toks * half * width, "decoder_grads", slots // g,
     )
 
 
 def local(acts, targets, enc_weight, enc_bias, gate_mask, dec_list, dec_weight):
-    layers, tok_rows, width_part = acts.shape
+    layers, tok_rows, width = acts.shape
     lat_dev = enc_weight.shape[1]
     slots, block, _ = dec_weight.shape
-    per_dev = lat_dev // block
-    n, w_count, r_count = lax.axis_size("lay"), lax.axis_size("wid"), lax.axis_size("rep")
-    lay, wid, rep = lax.axis_index("lay"), lax.axis_index("wid"), lax.axis_index("rep")
-    lat_total = lat_dev * n
-    blocks_total = lat_total // block
-    latents_layer = lat_total // layers
-    blocks_layer = latents_layer // block
-    toks = tok_rows // w_count
-
-    tgt = dec_list[:, 1]
-    valid = (tgt >= 0).astype(jnp.int32)
-    ids = jnp.maximum(dec_list[:, 0] * blocks_layer + dec_list[:, 2], 0)
-    tgt = jnp.maximum(tgt, 0)
-
-    here = lax.dynamic_index_in_dim(acts, lay * lat_dev // latents_layer, 0, keepdims=False)
-    here = here.reshape(w_count, toks, width_part)
+    w_count, r_count = lax.axis_size("wid"), lax.axis_size("rep")
+    shape = (layers, w_count, tok_rows // w_count, width)
     scale = float(tok_rows * r_count) ** (-0.5)
-    pre_mine, lat, lat_twin, err, err_twin, acts_all = step(
-        slot_tables(dec_list, layers, blocks_total, blocks_layer), here, enc_weight,
-        enc_bias.reshape(1, lat_dev), gate_mask.reshape(w_count, toks, per_dev), dec_weight,
-        targets.reshape(layers, w_count, toks, width_part), scale, 0,
+    tables, pre_mine, lat, err, acts_all = step(
+        acts.reshape(shape), enc_weight, enc_bias.reshape(1, lat_dev), gate_mask.T, dec_list.T,
+        dec_weight, targets.reshape(shape), scale, 0,
     )
     pre_all = [pre_mine] + [
         lax.ppermute(pre_mine, "wid", [(i, (i - d) % w_count) for i in range(w_count)])
         for d in range(1, w_count)
     ]
-    half = block // r_count
+    everyone = r_count * tok_rows
     dec_out = decoder_grads(
-        ids, tgt, valid, rep.reshape(1).astype(jnp.int32),
-        lat.reshape(blocks_total, tok_rows, block), lat_twin.reshape(blocks_total, tok_rows, half),
-        err.reshape(layers, tok_rows, width_part), err_twin.reshape(layers, tok_rows, width_part), slots,
+        tables, lat.reshape(lat.shape[0], everyone, block // r_count), err.reshape(layers, everyone, width),
+        slots,
     )
-    columns = lat_dev // r_count
-    pre_all = jnp.stack(pre_all).reshape(r_count * tok_rows, columns)
+    pre_all = jnp.stack(pre_all).reshape(everyone, lat_dev // r_count)
     enc_out = lax.dot_general(
-        acts_all.reshape(r_count * tok_rows, width_part), pre_all, (((0,), (0,)), ((), ())),
-        preferred_element_type=F32,
+        acts_all.reshape(everyone, width), pre_all, (((0,), (0,)), ((), ())), preferred_element_type=F32
     )
     bias_out = jnp.sum(pre_all.astype(F32), axis=0)
     return (enc_out, bias_out, dec_out)

time: 184 us -> 159 us (0.86)
  Pallas kernels: 169 us -> 152 us
  local copies, waits for them, and re-layouts: 4.73 us -> 0.01 us
  other arithmetic: 3.36 us -> 0.77 us
    pallas_call x2 -> x1, Pallas kernels: 156 us -> 140 us  [step(): pl.pallas_call(body, out_shape=(jax.ShapeDtypeStruct((at.size,), jnp.int3...]
    unnamed x4 -> x2, local copies, waits for them, and re-layouts: 2.86 us -> 0.01 us
    dynamic_slice x1 -> x0, local copies, waits for them, and re-layouts: 1.87 us -> none  [local(): lax.dynamic_index_in_dim(acts, lay * lat_dev // latents_layer, 0, keepdim...]
  transfers between devices with their start and end apart: 1 -> 1, of which waited for: 0 -> 1; matrix products, arithmetic and copies ran while one was open for 1% -> 0% of each run, Pallas kernels for 7% -> 8%
where the time goes in v4:
time: 159 us
  Pallas kernels  152 us (96%)
  matrix products  4.53 us (3%)
    pallas_call x1, Pallas kernels, step(): pl.pallas_call(body, out_shape=(jax.ShapeDtypeStruct((at.size,), jnp.int3...  140 us
    pallas_call x1, Pallas kernels, slot_call(): pl.pallas_call(body, out_shape=out_shape, grid_spec=pltpu.PrefetchScalarG...  12.6 us
    dot_general x1, matrix products, local(): lax.dot_general(acts_all.reshape(everyone, width), pre_all, (((0,), (0,))...  4.53 us
  transfers between devices with their start and end apart: 1, of which 1 were waited for; matrix products, arithmetic and copies ran while one was open for 0% of the time, Pallas kernels for 8%

profile of v4, /device:TPU:0, one launch (start us, length us, event | category | flops | bytes accessed | tf_op | source)
XLA Modules:
  0.0 159.0 jit_solution(12067242857078458454)
XLA Ops:
  0.6 139.5 %step.1 = (s32[256]{0:T(256)}, bf16[2,128,1024]{2,1,0:T(8,128)(2,1)}, bf16[32,2,2,128,128]{4,3,2,1,0:T(8,128)(2,1)}, bf16[4,2,2,128,1024]{4,3,2,1,0:T(8,128)(2,1)}, bf16[2,2,128,1024]{3,2,1,0:T(8,128)(2,1)}) custom-call(s32[3,21]{1,0:T(4,128)} %bitcast.24, bf16[4,2,128,1024]{3,2,1,0:T(8,128)(2,1)} %bitcast.16, bf16[1024,2048]{1,0:T(8,128)(2,1)} %ew_hbm.1, ...), custom_call_target="tpu_custom_call" | custom-call | tf_op jit(solution)/shard_map/step/pallas_call | solution.py:668
  140.1 0.5 collective-permute-start
  140.7 0.0 copy-start
  140.7 12.6 %decoder_grads.1 = f32[21,128,1024]{2,1,0:T(8,128)} custom-call(s32[256]{0:T(256)} %get-tuple-element.10.tab, bf16[32,512,128]{2,1,0:T(8,128)(2,1)} %bitcast.14, bf16[4,512,1024]{2,1,0:T(8,128)(2,1)} %bitcast.15), custom_call_target="tpu_custom_call" | custom-call | flops 2818572288 | bytes 19398656 | tf_op jit(solution)/shard_map/decoder_grads/pallas_call | solution.py:76
  153.3 0.4 collective-permute-done
  153.6 0.0 copy-done
  153.6 0.8 convert_reduce_fusion
  154.4 4.5 %convolution_bitcast_fusion = f32[1024,1024]{1,0:T(8,128)} fusion(bf16[2,2,128,1024]{3,2,1,0:T(8,128)(2,1)} %get-tuple-element.8, bf16[1,2,128,1024]{3,2,1,0:T(8,128)(2,1)S(1)} %bitcast.21, bf16[1,2,128,1024]{3,2,1,0:T(8,128)(2,1)S(1)} %bitcast.19), kind=kOutput, calls=%fused_computation | convolution fusion | flops 1074266112 | bytes 6291456 | tf_op jit(solution)/shard_map/dot_general | solution.py:763
Async XLA Ops:
  140.1 13.5 %collective-permute-start = (bf16[2,128,1024]{2,1,0:T(8,128)(2,1)}, bf16[2,128,1024]{2,1,0:T(8,128)(2,1)S(1)}, u32[]{:S(2)}, u32[]{:S(2)}) collective-permute-start(bf16[2,128,1024]{2,1,0:T(8,128)(2,1)} %get-tuple-element.9), channel_id=1, source_target_pairs={{0,2},{2,0},{1,3},{3,1},{4,6},{6,4},{5,7},{7,5},{8,10},{10,8},{9,1... | collective-permute-start | bytes 1572872 | tf_op jit(solution)/shard_map/ppermute | solution.py:754
  140.7 13.0 %copy-start = (bf16[2,128,1024]{2,1,0:T(8,128)(2,1)S(1)}, bf16[2,128,1024]{2,1,0:T(8,128)(2,1)}, u32[]{:S(2)}) copy-start(bf16[2,128,1024]{2,1,0:T(8,128)(2,1)} %get-tuple-element.9) | copy-start | bytes 1572868

commit v5 on v4

--- a/solution.py
+++ b/solution.py
@@ -10,13 +10,18 @@
 MESH = pl.DeviceIdType.MESH
 BF16 = jnp.bfloat16
 F32 = jnp.float32
+CHUNKS = 4
 CUTS = 2
 SKEW = 4
-Z_SKEW = 5
-PERIOD = 8
-A_GATE = 14
-A_SKEW = 3
-A_ACROSS = 7
+Z_SKEW = 4
+P_PERIOD = 5
+A_PERIOD = 9
+B_PERIOD = 9
+C_PERIOD = 7
+A_GATE = 9
+A_SKEW = 4
+A_ACROSS = 6
+B_ACROSS = 0
 C_ACROSS = 3
 
 
@@ -96,7 +101,7 @@
 
 
 def chunk_count(toks):
-    return next(c for c in (4, 2, 1) if toks % (16 * c) == 0 or c == 1)
+    return next(c for c in (CHUNKS, 4, 2, 1) if toks % (16 * c) == 0 or c == 1)
 
 
 def step(acts, enc_weight, enc_bias, gate, dec_list, dec_weight, targets, scale, cid):
@@ -115,6 +120,7 @@
     ct = toks // chunks
     rows = w_count * ct
     wide = min(lat_dev, 512)
+    cols = lat_dev // wide
 
     cuts = next(c for c in (CUTS, 1) if width % (128 * c) == 0)
     part = width // cuts
@@ -128,20 +134,20 @@
     g = group_of(slots)
     groups = slots // g
 
-    period = max(b_steps, z_steps, PERIOD)
-    per_step = -(-slots // period)
-    a_decode = A_GATE + A_SKEW * (n - 1) + A_ACROSS
-    b_first = a_decode + period
-    c_slots = b_first + b_steps + SKEW * (n - 1)
-    c_gather = c_slots + period + C_ACROSS
-    ticks = c_gather + (chunks - 1) * period + split + (n - 1) * max(split, Z_SKEW)
-
+    p_period, a_period = P_PERIOD, A_PERIOD
+    b_period, c_period = max(b_steps, B_PERIOD), max(z_steps, C_PERIOD)
+    per_step = -(-slots // b_period)
+    a_decode = A_GATE + A_SKEW * (n - 1) + A_ACROSS + max(0, a_period - b_period) * (chunks - 1)
+    b_first = a_decode + b_period
+    c_slots = b_first + b_steps - 1 + SKEW * (n - 1) + B_ACROSS + max(0, b_period - c_period) * (chunks - 1)
+    c_gather = c_slots + c_period + C_ACROSS
+    ticks = c_gather + (chunks - 1) * c_period + split + (n - 1) * max(split, Z_SKEW)
     table_slots = -(-slots // (a_decode - 1))
     table_blocks = -(-blocks // (a_decode - 1))
 
-    def body(d_ref, a_hbm, ew_hbm, b_ref, g_ref, w_hbm, t_ref,
+    def body(d_ref, a_hbm, ew_hbm, b_ref, g_ref, w_hbm, t_hbm,
              tab, po_ref, lo_ref, eo_ref, ao_ref,
-             a_ref, ew_ref, keep_ref, w_ref, lat_ref, lat_now, sl_ref, p_out, p_in, e_ref, sums, own_ref, bu_in, bd_in, bu_out, bd_out,
+             a_ref, ew_ref, keep_ref, t_ref, w_ref, lat_ref, lat_now, sl_ref, p_out, p_in, e_ref, sums, own_ref, bu_in, bd_in, bu_out, bd_out,
              x_out, x_in, c_sums, made, zu_in, zd_in, zu_out, zd_out, twin_out,
              wsem, ps, pr, aus, ads, azr, axs, axr, bus, bur, bds, bdr, xs, xr, zus, zur, zds, zdr,
              ts, tr, tps, tpr, asem, isem):
@@ -160,7 +166,9 @@
         acts_in.start()
         for copy in enc_in:
             copy.start()
+        aims = pltpu.make_async_copy(t_hbm, t_ref, isem.at[1 + lat_dev // wide])
         loop(0, slots, lambda k: weight(k).start())
+        aims.start()
         barrier = pltpu.get_barrier_semaphore()
         others(l, n, lambda j: signal(barrier, lay=j))
         others(w, w_count, lambda v: signal(barrier, wid=v))
@@ -216,33 +224,36 @@
         def chunk(c):
             return pl.ds(pl.multiple_of(c * ct, ct), ct)
 
-        def at_chunk(s, first, do, last=0):
+        def at_chunk(s, first, period, do):
             t = s - first
 
             @pl.when((t >= 0) & (t < chunks * period))
             def _():
-                @pl.when(lax.rem(t, period) == last)
+                @pl.when(lax.rem(t, period) == 0)
                 def _():
                     do(t // period)
 
 
-        def p_send(c, v):
-            return remote(p_out.at[c, v], p_in.at[c, w], ps.at[c * w_count + v], pr.at[c * w_count + w], wid=v)
-
-        def p_landed(c, v):
-            return remote(p_in.at[c, v], p_in.at[c, v], ps.at[c * w_count + v], pr.at[c * w_count + v], wid=v)
+        def p_send(c, i, v):
+            over, q = pl.ds(i * wide, wide), (c * cols + i) * w_count
+            return remote(p_out.at[c, v, :, over], p_in.at[c, w, :, over], ps.at[q + v], pr.at[q + w], wid=v)
+
+        def p_landed(c, i, v):
+            over, q = pl.ds(i * wide, wide), (c * cols + i) * w_count
+            return remote(p_in.at[c, v, :, over], p_in.at[c, v, :, over], ps.at[q + v], pr.at[q + v], wid=v)
 
         def product(c):
             held = a_ref[:, chunk(c), :].reshape(rows, width)
-            for i, o in enumerate(range(0, lat_dev, wide)):
+            for i in range(cols):
                 @pl.when(c == 0)
                 def _():
                     enc_in[i].wait()
 
-                made_here = jnp.dot(held, ew_ref[:, o:o + wide], preferred_element_type=F32).astype(BF16)
+                over = slice(i * wide, (i + 1) * wide)
+                made_here = jnp.dot(held, ew_ref[:, over], preferred_element_type=F32).astype(BF16)
                 for v in range(w_count):
-                    p_out[c, v, :, o:o + wide] = made_here[v * ct:(v + 1) * ct]
-            others(w, w_count, lambda v: p_send(c, v).start())
+                    p_out[c, v, :, over] = made_here[v * ct:(v + 1) * ct]
+                others(w, w_count, lambda v: p_send(c, i, v).start())
 
         def shard(c, j, v):
             return lat_ref.at[pl.ds(j * per_dev, per_dev), v, chunk(c)]
@@ -269,7 +280,8 @@
             others(w, w_count, lambda v: do(across(c, j, v, w)))
 
         def gated(c):
-            others(w, w_count, lambda v: p_landed(c, v).wait_recv())
+            for i in range(cols):
+                others(w, w_count, lambda v: p_landed(c, i, v).wait_recv())
             keep = keep_ref[pl.ds(pl.multiple_of(w * toks + c * ct, ct), ct), :]
             for b in range(per_dev):
                 over = slice(b * block, (b + 1) * block)
@@ -307,10 +319,10 @@
             return remote(bd_out.at[q], bd_in.at[q], bds.at[q], bdr.at[q], lay=l - 1)
 
         def b_inside(q):
-            return (q >= 0) & (q < chunks * period) & (lax.rem(q + period * chunks, period) < b_steps)
+            return (q >= 0) & (q < chunks * b_period) & (lax.rem(q + b_period * chunks, b_period) < b_steps)
 
         def b_piece(q):
-            return q // period * b_steps + lax.rem(q + period * chunks, period)
+            return q // b_period * b_steps + lax.rem(q + b_period * chunks, b_period)
 
         def hand_on(s):
             q, p = s - SKEW * l, s - SKEW * (n - 1 - l)
@@ -420,10 +432,10 @@
             return remote(zd_out.at[q], zd_in.at[q], zds.at[q], zdr.at[q], lay=l - 1)
 
         def z_inside(q):
-            return (q >= 0) & (q < chunks * period) & (lax.rem(q + period * chunks, period) < z_steps)
+            return (q >= 0) & (q < chunks * c_period) & (lax.rem(q + c_period * chunks, c_period) < z_steps)
 
         def z_piece(q):
-            return q // period * z_steps + lax.rem(q + period * chunks, period)
+            return q // c_period * z_steps + lax.rem(q + c_period * chunks, c_period)
 
         def own_z(q, dest):
             return made[q // z_steps, pl.ds(dest * per_dev + lax.rem(q, split) * pb, pb)].astype(F32)
@@ -468,9 +480,9 @@
             off_up = (n - 1 - l) * split
             off_dn = l * split
             f = s - jnp.maximum(off_up + Z_SKEW * l, off_dn + Z_SKEW * (n - 1 - l))
-            i = lax.rem(f + period * chunks, period)
-            whole = (f >= 0) & (f < chunks * period) & (i < split)
-            c = f // period
+            i = lax.rem(f + c_period * chunks, c_period)
+            whole = (f >= 0) & (f < chunks * c_period) & (i < split)
+            c = f // c_period
 
             def finish(total):
                 blocks_here = pl.ds(i * pb, pb)
@@ -548,14 +560,14 @@
 
         def tick(s, carry):
             def arrive(d):
-                at_chunk(s, A_GATE + A_SKEW * d, lambda c: nearest(l, n, d, lambda j: take(c, j)))
+                at_chunk(s, A_GATE + A_SKEW * d, a_period, lambda c: nearest(l, n, d, lambda j: take(c, j)))
 
             loop(1, n, arrive)
             hand_on(s - b_first)
-            at_chunk(s, c_gather, gather)
+            at_chunk(s, c_gather, c_period, gather)
             reduce_on(s - c_gather)
-            at_chunk(s, A_GATE, gated)
-            at_chunk(s, 0, product)
+            at_chunk(s, A_GATE, a_period, gated)
+            at_chunk(s, 0, p_period, product)
 
             @pl.when(s < a_decode - 1)
             def _():
@@ -563,19 +575,19 @@
 
             t = s - c_slots
 
-            @pl.when((t >= 0) & (t < chunks * period))
-            def _():
-                c, i = t // period, lax.rem(t, period)
+            @pl.when((t >= 0) & (t < chunks * c_period))
+            def _():
+                c, i = t // c_period, lax.rem(t, c_period)
                 lax.fori_loop(
-                    (i * groups + period - 1) // period, ((i + 1) * groups + period - 1) // period,
+                    (i * groups + c_period - 1) // c_period, ((i + 1) * groups + c_period - 1) // c_period,
                     lambda j, z: (slot_group(c, j), z)[1], 0,
                 )
 
             u = s - a_decode
 
-            @pl.when((u >= 0) & (u < chunks * period))
-            def _():
-                c, i = u // period, lax.rem(u, period)
+            @pl.when((u >= 0) & (u < chunks * b_period))
+            def _():
+                c, i = u // b_period, lax.rem(u, b_period)
 
                 @pl.when(i == 0)
                 def _():
@@ -586,23 +598,24 @@
                     def _():
                         slot(i * per_step + d)
 
-                @pl.when(i == period - 1)
+                @pl.when(i == b_period - 1)
                 def _():
                     emit(c)
 
             @pl.when(s == a_decode - 1)
             def _():
                 loop(0, slots, lambda k: weight(k).wait())
+                aims.wait()
                 for v in range(w_count):
                     twins[2 + v].start()
                     mine[2 + v].start()
 
-            @pl.when(s == a_decode + (chunks - 1) * period)
+            @pl.when(s == a_decode + (chunks - 1) * b_period)
             def _():
                 twins[0].start()
                 mine[0].start()
 
-            @pl.when(s == c_slots + (chunks - 1) * period)
+            @pl.when(s == c_slots + (chunks - 1) * c_period)
             def _():
                 twins[1].start()
                 mine[1].start()
@@ -652,7 +665,8 @@
 
         lax.fori_loop(0, chunks * groups, x_sent, 0)
         for c in range(chunks):
-            others(w, w_count, lambda v: p_send(c, v).wait_send())
+            for i in range(cols):
+                others(w, w_count, lambda v: p_send(c, i, v).wait_send())
             twin_landed(c).wait()
         for copy in twins + mine:
             copy.wait()
@@ -674,12 +688,13 @@
             jax.ShapeDtypeStruct((layers, r_count, w_count, toks, width), BF16),
             jax.ShapeDtypeStruct((w_count, r_count, toks, width), BF16),
         ),
-        in_specs=[smem, ANY, ANY, vmem, vmem, ANY, vmem],
+        in_specs=[smem, ANY, ANY, vmem, vmem, ANY, ANY],
         out_specs=(smem, vmem, ANY, ANY, ANY),
         scratch_shapes=[
             pltpu.VMEM((w_count, toks, width), BF16),
             pltpu.VMEM(enc_weight.shape, BF16),
             pltpu.VMEM((w_count * toks, per_dev), F32),
+            pltpu.VMEM(targets.shape, BF16),
             pltpu.VMEM(dec_weight.shape, BF16),
             pltpu.VMEM(lat_shape, BF16),
             pltpu.VMEM((blocks, w_count, ct, block), BF16),
@@ -695,11 +710,11 @@
             pltpu.VMEM((chunks, blocks, ct, block), BF16),
         ] + [pltpu.VMEM(z_piece_shape, BF16)] * 4 + [
             pltpu.VMEM((chunks, ct, columns), BF16),
-            dma((slots,)), dma((chunks * w_count,)), dma((chunks * w_count,)),
+            dma((slots,)), dma((chunks * cols * w_count,)), dma((chunks * cols * w_count,)),
         ] + [dma((chunks * n,))] * 3 + [dma((chunks * n * w_count,))] * 2 + [dma((b_pieces,))] * 4
         + [dma((x_sems,))] * 2 + [dma((z_pieces,))] * 4 + [
             dma((2 + w_count,)), dma((2 + w_count,)), dma((chunks,)), dma((chunks,)), dma((2 + w_count,)),
-            dma((1 + lat_dev // wide,)),
+            dma((2 + lat_dev // wide,)),
         ],
         compiler_params=pltpu.CompilerParams(
             collective_id=cid, has_side_effects=True, vmem_limit_bytes=67043328

time: 159 us -> 156 us (0.981)
  Pallas kernels: 152 us -> 150 us
    pallas_call x1, Pallas kernels: 140 us -> 137 us  [step(): pl.pallas_call(body, out_shape=(jax.ShapeDtypeStruct((at.size,), jnp.int3...]
where the time goes in v5:
time: 156 us
  Pallas kernels  150 us (96%)
  matrix products  4.53 us (3%)
    pallas_call x1, Pallas kernels, step(): pl.pallas_call(body, out_shape=(jax.ShapeDtypeStruct((at.size,), jnp.int3...  137 us
    pallas_call x1, Pallas kernels, slot_call(): pl.pallas_call(body, out_shape=out_shape, grid_spec=pltpu.PrefetchScalarG...  13 us
    dot_general x1, matrix products, local(): lax.dot_general(acts_all.reshape(everyone, width), pre_all, (((0,), (0,))...  4.53 us
  transfers between devices with their start and end apart: 1, of which 1 were waited for; matrix products, arithmetic and copies ran while one was open for 0% of the time, Pallas kernels for 8%

profile of v5, /device:TPU:0, one launch (start us, length us, event | category | flops | bytes accessed | tf_op | source)
XLA Modules:
  0.0 156.2 jit_solution(13800432338573699036)
XLA Ops:
  0.6 136.7 %step.1 = (s32[256]{0:T(256)}, bf16[2,128,1024]{2,1,0:T(8,128)(2,1)}, bf16[32,2,2,128,128]{4,3,2,1,0:T(8,128)(2,1)}, bf16[4,2,2,128,1024]{4,3,2,1,0:T(8,128)(2,1)}, bf16[2,2,128,1024]{3,2,1,0:T(8,128)(2,1)}) custom-call(s32[3,21]{1,0:T(4,128)} %bitcast.24, bf16[4,2,128,1024]{3,2,1,0:T(8,128)(2,1)} %bitcast.16, bf16[1024,2048]{1,0:T(8,128)(2,1)} %ew_hbm.1, ...), custom_call_target="tpu_custom_call" | custom-call | tf_op jit(solution)/shard_map/step/pallas_call | solution.py:682
  137.4 0.4 collective-permute-start
  137.8 0.0 copy-start
  137.8 13.0 %decoder_grads.1 = f32[21,128,1024]{2,1,0:T(8,128)} custom-call(s32[256]{0:T(256)} %get-tuple-element.10.tab, bf16[32,512,128]{2,1,0:T(8,128)(2,1)} %bitcast.14, bf16[4,512,1024]{2,1,0:T(8,128)(2,1)} %bitcast.15), custom_call_target="tpu_custom_call" | custom-call | flops 2818572288 | bytes 19398656 | tf_op jit(solution)/shard_map/decoder_grads/pallas_call | solution.py:81
  150.8 0.1 collective-permute-done
  150.9 0.0 copy-done
  150.9 0.8 convert_reduce_fusion
  151.7 4.5 %convolution_bitcast_fusion = f32[1024,1024]{1,0:T(8,128)} fusion(bf16[2,2,128,1024]{3,2,1,0:T(8,128)(2,1)} %get-tuple-element.8, bf16[1,2,128,1024]{3,2,1,0:T(8,128)(2,1)S(1)} %bitcast.21, bf16[1,2,128,1024]{3,2,1,0:T(8,128)(2,1)S(1)} %bitcast.19), kind=kOutput, calls=%fused_computation | convolution fusion | flops 1074266112 | bytes 6291456 | tf_op jit(solution)/shard_map/dot_general | solution.py:778
Async XLA Ops:
  137.4 13.5 %collective-permute-start = (bf16[2,128,1024]{2,1,0:T(8,128)(2,1)}, bf16[2,128,1024]{2,1,0:T(8,128)(2,1)S(1)}, u32[]{:S(2)}, u32[]{:S(2)}) collective-permute-start(bf16[2,128,1024]{2,1,0:T(8,128)(2,1)} %get-tuple-element.9), channel_id=1, source_target_pairs={{0,2},{2,0},{1,3},{3,1},{4,6},{6,4},{5,7},{7,5},{8,10},{10,8},{9,1... | collective-permute-start | bytes 1572872 | tf_op jit(solution)/shard_map/ppermute | solution.py:769
  137.8 13.1 %copy-start = (bf16[2,128,1024]{2,1,0:T(8,128)(2,1)S(1)}, bf16[2,128,1024]{2,1,0:T(8,128)(2,1)}, u32[]{:S(2)}) copy-start(bf16[2,128,1024]{2,1,0:T(8,128)(2,1)} %get-tuple-element.9) | copy-start | bytes 1572868

commit v6 on v5

--- a/solution.py
+++ b/solution.py
@@ -16,13 +16,13 @@
 Z_SKEW = 4
 P_PERIOD = 5
 A_PERIOD = 9
-B_PERIOD = 9
+B_PERIOD = 8
 C_PERIOD = 7
 A_GATE = 9
 A_SKEW = 4
-A_ACROSS = 6
+A_ACROSS = 4
 B_ACROSS = 0
-C_ACROSS = 3
+C_ACROSS = 2
 
 
 def smooth_gate(shifted):

time: 156 us -> 156 us (level)
  transfers between devices with their start and end apart: 1 -> 1, of which waited for: 1 -> 0; matrix products, arithmetic and copies ran while one was open for 0% -> 0% of each run, Pallas kernels for 8% -> 8%
where the time goes in v6:
time: 156 us
  Pallas kernels  149 us (96%)
  matrix products  4.53 us (3%)
    pallas_call x1, Pallas kernels, step(): pl.pallas_call(body, out_shape=(jax.ShapeDtypeStruct((at.size,), jnp.int3...  136 us
    pallas_call x1, Pallas kernels, slot_call(): pl.pallas_call(body, out_shape=out_shape, grid_spec=pltpu.PrefetchScalarG...  13 us
    dot_general x1, matrix products, local(): lax.dot_general(acts_all.reshape(everyone, width), pre_all, (((0,), (0,))...  4.53 us
  transfers between devices with their start and end apart: 1, of which 0 were waited for; matrix products, arithmetic and copies ran while one was open for 0% of the time, Pallas kernels for 8%

profile of v6, /device:TPU:0, one launch (start us, length us, event | category | flops | bytes accessed | tf_op | source)
XLA Modules:
  0.0 155.8 jit_solution(4178437413953128447)
XLA Ops:
  0.6 136.3 %step.1 = (s32[256]{0:T(256)}, bf16[2,128,1024]{2,1,0:T(8,128)(2,1)}, bf16[32,2,2,128,128]{4,3,2,1,0:T(8,128)(2,1)}, bf16[4,2,2,128,1024]{4,3,2,1,0:T(8,128)(2,1)}, bf16[2,2,128,1024]{3,2,1,0:T(8,128)(2,1)}) custom-call(s32[3,21]{1,0:T(4,128)} %bitcast.24, bf16[4,2,128,1024]{3,2,1,0:T(8,128)(2,1)} %bitcast.16, bf16[1024,2048]{1,0:T(8,128)(2,1)} %ew_hbm.1, ...), custom_call_target="tpu_custom_call" | custom-call | tf_op jit(solution)/shard_map/step/pallas_call | solution.py:682
  136.9 0.6 collective-permute-start
  137.6 0.0 copy-start
  137.6 13.0 %decoder_grads.1 = f32[21,128,1024]{2,1,0:T(8,128)} custom-call(s32[256]{0:T(256)} %get-tuple-element.10.tab, bf16[32,512,128]{2,1,0:T(8,128)(2,1)} %bitcast.14, bf16[4,512,1024]{2,1,0:T(8,128)(2,1)} %bitcast.15), custom_call_target="tpu_custom_call" | custom-call | flops 2818572288 | bytes 19398656 | tf_op jit(solution)/shard_map/decoder_grads/pallas_call | solution.py:81
  150.5 0.0 collective-permute-done
  150.5 0.0 copy-done
  150.5 0.8 convert_reduce_fusion
  151.3 4.5 %convolution_bitcast_fusion = f32[1024,1024]{1,0:T(8,128)} fusion(bf16[2,2,128,1024]{3,2,1,0:T(8,128)(2,1)} %get-tuple-element.8, bf16[1,2,128,1024]{3,2,1,0:T(8,128)(2,1)S(1)} %bitcast.21, bf16[1,2,128,1024]{3,2,1,0:T(8,128)(2,1)S(1)} %bitcast.19), kind=kOutput, calls=%fused_computation | convolution fusion | flops 1074266112 | bytes 6291456 | tf_op jit(solution)/shard_map/dot_general | solution.py:778
Async XLA Ops:
  136.9 13.6 %collective-permute-start = (bf16[2,128,1024]{2,1,0:T(8,128)(2,1)}, bf16[2,128,1024]{2,1,0:T(8,128)(2,1)S(1)}, u32[]{:S(2)}, u32[]{:S(2)}) collective-permute-start(bf16[2,128,1024]{2,1,0:T(8,128)(2,1)} %get-tuple-element.9), channel_id=1, source_target_pairs={{0,2},{2,0},{1,3},{3,1},{4,6},{6,4},{5,7},{7,5},{8,10},{10,8},{9,1... | collective-permute-start | bytes 1572872 | tf_op jit(solution)/shard_map/ppermute | solution.py:769
  137.6 13.0 %copy-start = (bf16[2,128,1024]{2,1,0:T(8,128)(2,1)S(1)}, bf16[2,128,1024]{2,1,0:T(8,128)(2,1)}, u32[]{:S(2)}) copy-start(bf16[2,128,1024]{2,1,0:T(8,128)(2,1)} %get-tuple-element.9) | copy-start | bytes 1572868
